TPU v7x, 256 devices: a 8x8x2 block of a 8x8x16 slice. The times are simulated.
256 devices in a mesh: band: 2 (over z), tm: 128 (over x, y, core).
Axes of the slice: x: 8, y: 8, z: 2, core: 2. Of those that a mesh axis runs over, the one named last changes fastest.
The devices are a block of a 8x8x16 slice.
Arguments:
- volts: int32 [8, 2, 25165824], P('band', None, 'tm'), parts along dimension 0, may hold values from -128 to 127, as said below
- taps: float32 [16, 4096], replicated, may hold values from -0.024 to 0.024
- pairs: int32 [4, 2], replicated, may hold values from 0 to 3, as said below
Outputs:
- coherence: float32 [8, 4096], P('band'), parts along dimension 0
- normalized: float32 [2, 8, 6144, 4096], P(None, 'band', 'tm'), parts along dimension 1
There are 2 independent parts, one for each index of `band`. A program takes and returns all parts, laid end to end along the dimension named above; an argument that names none is the same for every part. Nothing has to cross between parts.
Inputs may be any that keep to these rules, and one draw needn't show every extreme that they name: `volts`: every sample is a whole number of the int8 range. Each pair names a stream of the first antenna (0 or 1) and then one of the second antenna (2 or 3); the four pairs are distinct.
All inputs are finite; a program needn't handle non-finite values.
Results may differ from a plain program's by a relative error of at most 0.000067.
Values sent between devices are 32-bit elements; how exact they have to be, the bound alone decides.
A program may use at most 128 MiB of HBM per device.

v0:
```python
import functools
import math

import jax
import jax.numpy as jnp
import numpy as np
from jax import lax
from jax.experimental import pallas as pl
from jax.experimental.pallas import tpu as pltpu
from jax.sharding import Mesh
from jax.sharding import PartitionSpec as P

TM = ("tm_0", "tm_1", "tm_2")
ROWS = 32
LANES = 128
PITCH = 65
HALO = 16
GROUP = 8


def constants():
    lane = np.arange(LANES)
    j = 4 * (lane % 32) + lane // 32
    k = np.arange(LANES)
    angle = 2.0 * np.pi * ((j[:, None] * k[None, :]) % LANES) / LANES
    cos, sin = np.cos(angle) / 64.0, np.sin(angle) / 64.0
    full = np.block([[cos, -sin], [sin, cos]]).astype(np.float32)
    high = full.astype(jnp.bfloat16)
    low = (full - high.astype(np.float32)).astype(jnp.bfloat16)
    i = np.arange(ROWS)
    turn = 2.0 * np.pi * ((i[:, None] * k[None, :]) % 4096) / 4096
    return (
        high,
        low,
        np.cos(turn).astype(np.float32),
        np.sin(turn).astype(np.float32),
    )


def add(a, b):
    return (a[0] + b[0], a[1] + b[1])


def sub(a, b):
    return (a[0] - b[0], a[1] - b[1])


def fft4(x):
    a, b = add(x[0], x[2]), sub(x[0], x[2])
    c, d = add(x[1], x[3]), sub(x[1], x[3])
    return [
        add(a, c),
        (b[0] + d[1], b[1] - d[0]),
        sub(a, c),
        (b[0] - d[1], b[1] + d[0]),
    ]


def fft8(x):
    even = fft4(x[0::2])
    odd = fft4(x[1::2])
    r = np.float32(math.sqrt(0.5))
    turned = [
        odd[0],
        ((odd[1][0] + odd[1][1]) * r, (odd[1][1] - odd[1][0]) * r),
        (odd[2][1], -odd[2][0]),
        ((odd[3][1] - odd[3][0]) * r, (odd[3][0] + odd[3][1]) * -r),
    ]
    return [add(e, o) for e, o in zip(even, turned)] + [sub(e, o) for e, o in zip(even, turned)]


def rotate(x, index, length):
    index = index % length
    if index == 0:
        return x
    if index * 4 == length:
        return (x[1], -x[0])
    c = np.float32(math.cos(2 * math.pi * index / length))
    s = np.float32(math.sin(2 * math.pi * index / length))
    return (x[0] * c + x[1] * s, x[1] * c - x[0] * s)


def block_transpose(rows):
    turned = rows.T
    lane = lax.broadcasted_iota(jnp.int32, (32, LANES), 1)
    odd = (lane & 32) != 0
    upper = (lane & 64) != 0
    r = [turned[32 * b : 32 * b + 32] for b in range(4)]

    def pair(a, b, by, mask):
        return (
            jnp.where(mask, pltpu.roll(b, by, 1), a),
            jnp.where(mask, b, pltpu.roll(a, LANES - by, 1)),
        )

    a0, a1 = pair(r[0], r[1], 32, odd)
    b0, b1 = pair(r[2], r[3], 32, odd)
    o0, o2 = pair(a0, b0, 64, upper)
    o1, o3 = pair(a1, b1, 64, upper)
    return [o0, o1, o2, o3]


def permute_taps(taps_ref, tapb):
    def batch(tb, carry):
        high = tb // 2
        parts = [
            taps_ref[pl.ds(high * 256 + (tb % 2) * 4 + q, 32, stride=8), :] for q in range(4)
        ]
        out = block_transpose(jnp.concatenate(parts, axis=0))
        for q in range(4):
            for i in range(ROWS):
                tapb[pl.ds(pl.multiple_of((i * 16 + tb * 4 + q) * 8, 8), 8), :] = jnp.broadcast_to(
                    out[q][i : i + 1], (8, LANES)
                )
        return carry

    lax.fori_loop(0, 4, batch, 0)


def permute_samples(raw, xf, frame0, row0, batches):
    def batch(b, carry):
        for c in range(2):
            x = [raw[s, pl.ds((frame0 + 4 * b) * 64 + c, LANES, stride=2), :] for s in range(4)]
            packed = (
                (x[0] & 255)
                | ((x[1] & 255) << 8)
                | ((x[2] & 255) << 16)
                | (x[3] << 24)
            )
            out = block_transpose(packed)
            for q in range(4):
                for s in range(4):
                    value = out[q] << (24 - 8 * s) if s < 3 else out[q]
                    value = (value >> 24).astype(jnp.float32)
                    xf[2 * s + c, pl.ds(row0 + 4 * b + q, 32, stride=PITCH), :] = value
        return carry

    lax.fori_loop(0, batches, batch, 0)


def process_group(group, refs):
    (xf, tapb, wh, wl, twc, tws, yh, yl, v, u, pbuf, sums) = refs

    def fir(i, carry):
        base = i * PITCH + HALO + group * GROUP
        tap = [
            tapb[pl.ds(pl.multiple_of((i * 16 + t) * 8, 8), 8), :] for t in range(16)
        ]
        for c in range(2):
            for pair in range(2):
                ys = []
                for s in (2 * pair, 2 * pair + 1):
                    acc = None
                    for t in range(16):
                        term = tap[t] * xf[2 * s + c, pl.ds(base - t, 8), :]
                        acc = term if acc is None else acc + term
                    ys.append(acc)
                y = jnp.concatenate(ys, axis=0)
                high = y.astype(jnp.bfloat16)
                low = (y - high.astype(jnp.float32)).astype(jnp.bfloat16)
                at = pl.ds(pl.multiple_of(i * 32 + pair * 16, 16), 16)
                yh[at, c * LANES : (c + 1) * LANES] = high
                yl[at, c * LANES : (c + 1) * LANES] = low
        return carry

    lax.fori_loop(0, ROWS, fir, 0)

    def stage1(m, carry):
        at = pl.ds(pl.multiple_of(m * 256, 256), 256)
        h, l = yh[at, :], yl[at, :]
        dot = functools.partial(jnp.dot, preferred_element_type=jnp.float32)
        v[at, :] = dot(h, wh[...]) + dot(l, wh[...]) + dot(h, wl[...])
        return carry

    lax.fori_loop(0, 4, stage1, 0)

    def stage2a(s, carry):
        for i0 in range(4):
            xs = []
            for i1 in range(8):
                i = 4 * i1 + i0
                at = pl.ds(pl.multiple_of(i * 32 + s * 8, 8), 8)
                x = (v[at, :LANES], v[at, LANES:])
                if i:
                    c = twc[pl.ds(i, 8, stride=0), :] if False else jnp.broadcast_to(twc[i : i + 1, :], (8, LANES))
                    d = jnp.broadcast_to(tws[i : i + 1, :], (8, LANES))
                    x = (x[0] * c + x[1] * d, x[1] * c - x[0] * d)
                xs.append(x)
            for ka, x in enumerate(fft8(xs)):
                x = rotate(x, i0 * ka, 32)
                at = pl.ds(pl.multiple_of((s * 32 + i0 * 8 + ka) * 8, 8), 8)
                u[0, at, :] = x[0]
                u[1, at, :] = x[1]
        return carry

    lax.fori_loop(0, 4, stage2a, 0)

    def stage2b(ka, carry):
        spectra = []
        for s in range(4):
            xs = []
            for i0 in range(4):
                at = pl.ds(pl.multiple_of((s * 32 + i0 * 8 + ka) * 8, 8), 8)
                xs.append((u[0, at, :], u[1, at, :]))
            spectra.append(fft4(xs))
        for kb in range(4):
            k1 = ka + 8 * kb
            z = [spectra[s][kb] for s in range(4)]
            at = pl.ds(pl.multiple_of(k1 * 8, 8), 8)
            for s in range(4):
                sums[s, at, :] += z[s][0] * z[s][0] + z[s][1] * z[s][1]
            rows = pl.ds(pl.multiple_of(group * GROUP, 8), 8)
            cols = pl.ds(pl.multiple_of(k1 * LANES, LANES), LANES)
            for p in range(4):
                a, b = z[p // 2], z[2 + p % 2]
                re = a[0] * b[0] + a[1] * b[1]
                im = a[1] * b[0] - a[0] * b[1]
                sums[4 + p, at, :] += re
                sums[8 + p, at, :] += im
                pbuf[0, p, rows, cols] = re
                pbuf[1, p, rows, cols] = im
        return carry

    lax.fori_loop(0, 8, stage2b, 0)


def transform_kernel(
    samples_ref, halo_ref, taps_ref, wh, wl, twc, tws, prod_ref, sums_ref,
    xf, tapb, yh, yl, v, u, pbuf, sums, sems,
):
    refs = (xf, tapb, wh, wl, twc, tws, yh, yl, v, u, pbuf, sums)
    sums[...] = jnp.zeros_like(sums)
    permute_taps(taps_ref, tapb)
    permute_samples(samples_ref, xf, 0, HALO, 12)
    permute_samples(halo_ref, xf, 0, 0, 4)

    def out_copy(group):
        rows = pl.ds(pl.multiple_of(group * GROUP, 8), 8)
        return pltpu.make_async_copy(
            pbuf.at[:, :, rows, :], prod_ref.at[:, :, rows, :], sems.at[group]
        )

    def step(n, carry):
        group = lax.rem(n + 2, 6)
        process_group(group, refs)
        out_copy(group).start()
        return carry

    lax.fori_loop(0, 6, step, 0)
    for q in range(12):
        for k1 in range(ROWS):
            sums_ref[q, k1 : k1 + 1, :] = jnp.sum(
                sums[q, k1 * 8 : k1 * 8 + 8, :], axis=0, keepdims=True
            )
    for group in range(6):
        out_copy(group).wait()


def transform_call(rows, halo, taps_rows, interpret=False):
    streams = rows.shape[0]
    frames = rows.shape[1] // 64
    consts = [jnp.asarray(c) for c in constants()]
    vmem = pl.BlockSpec(memory_space=pltpu.VMEM)
    f32, bf16 = jnp.float32, jnp.bfloat16
    return pl.pallas_call(
        transform_kernel,
        out_shape=(
            jax.ShapeDtypeStruct((2, 4, frames, 4096), f32),
            jax.ShapeDtypeStruct((12, ROWS, LANES), f32),
        ),
        in_specs=[vmem] * 7,
        out_specs=(pl.BlockSpec(memory_space=pl.ANY), vmem),
        scratch_shapes=[
            pltpu.VMEM((8, ROWS * PITCH + 7, LANES), f32),
            pltpu.VMEM((ROWS * 16 * 8, LANES), f32),
            pltpu.VMEM((1024, 256), bf16),
            pltpu.VMEM((1024, 256), bf16),
            pltpu.VMEM((1024, 256), f32),
            pltpu.VMEM((2, 1024, LANES), f32),
            pltpu.VMEM((2, 4, frames, 4096), f32),
            pltpu.VMEM((12, ROWS * 8, LANES), f32),
            pltpu.SemaphoreType.DMA((6,)),
        ],
        compiler_params=pltpu.CompilerParams(vmem_limit_bytes=60 * 1024 * 1024),
        cost_estimate=pl.CostEstimate(flops=4_000_000_000, bytes_accessed=16_000_000, transcendentals=0),
        interpret=interpret,
        name="transform",
    )(rows, halo, taps_rows, *consts)


def normalize_kernel(total, canon_ref, pairs_ref, sums_ref, prod_ref, coh_ref, out_ref):
    pair = pl.program_id(0)
    canon = canon_ref[pair]
    first = pairs_ref[pair, 0]
    second = pairs_ref[pair, 1]
    scale = np.float32(1.0 / total)
    power = (sums_ref[first] * scale + 1e-06) * (sums_ref[second] * scale + 1e-06)
    factor = 1.0 / jnp.sqrt(power)

    @pl.when(pl.program_id(1) == 0)
    def _():
        re = sums_ref[4 + canon] * scale
        im = sums_ref[8 + canon] * scale
        coh_ref[0] = (re * re + im * im) / power

    for k1 in range(ROWS):
        cols = slice(k1 * LANES, (k1 + 1) * LANES)
        row = factor[k1 : k1 + 1]
        for part in range(2):
            out_ref[part, 0, :, cols] = prod_ref[part, 0, :, cols] * row


def normalize_call(pairs, sums, prods, total, block=24, interpret=False):
    frames = prods.shape[2]
    canon = pairs[:, 0] * 2 + pairs[:, 1] - 2
    f32 = jnp.float32
    coh, normalized = pl.pallas_call(
        functools.partial(normalize_kernel, total),
        grid_spec=pltpu.PrefetchScalarGridSpec(
            num_scalar_prefetch=2,
            grid=(4, frames // block),
            in_specs=[
                pl.BlockSpec((12, ROWS, LANES), lambda p, b, canon, pairs: (0, 0, 0)),
                pl.BlockSpec((2, 1, block, 4096), lambda p, b, canon, pairs: (0, canon[p], b, 0)),
            ],
            out_specs=[
                pl.BlockSpec((1, ROWS, LANES), lambda p, b, canon, pairs: (p, 0, 0)),
                pl.BlockSpec((2, 1, block, 4096), lambda p, b, canon, pairs: (0, p, b, 0)),
            ],
        ),
        out_shape=(
            jax.ShapeDtypeStruct((4, ROWS, LANES), f32),
            jax.ShapeDtypeStruct(prods.shape, f32),
        ),
        cost_estimate=pl.CostEstimate(flops=2_000_000, bytes_accessed=13_000_000, transcendentals=0),
        interpret=interpret,
        name="normalize",
    )(canon, pairs, sums, prods)
    return coh.reshape(4, ROWS * LANES), normalized


def sample_rows(volts):
    streams, comps, local = volts.shape
    rows = volts.reshape(streams, comps, local // LANES, LANES)
    return jnp.transpose(rows, (0, 2, 1, 3)).reshape(streams, local // LANES * comps, LANES)


def tap_rows(taps):
    taps = taps.reshape(2, 8, ROWS, LANES)
    return jnp.transpose(taps, (0, 2, 1, 3)).reshape(512, LANES)


def shifted(array, axis, by):
    devices = lax.axis_size(axis)
    pairs = [(i, i + by) for i in range(devices) if 0 <= i + by < devices]
    return lax.ppermute(array, axis, pairs)


def on_device(volts, taps, pairs):
    rows = sample_rows(volts)
    frames = rows.shape[1] // 64
    halo = shifted(rows[:, (frames - HALO) * 64 :], TM, 1)
    prods, sums = transform_call(rows, halo, tap_rows(taps))
    for axis in TM:
        sums = lax.psum(sums, axis)
    total = frames * lax.axis_size(TM)
    return normalize_call(pairs, sums, prods, total)


def solution(mesh):
    devices = mesh.devices
    finer = Mesh(
        devices.reshape(mesh.shape["band"], 8, 8, 2), ("band", "tm_0", "tm_1", "tm_2")
    )
    return jax.shard_map(
        on_device,
        mesh=finer,
        in_specs=(P("band", None, TM), P(), P()),
        out_specs=(P("band", None), P(None, "band", TM, None)),
        check_vma=False,
    )
```

profile of v0, /device:TPU:513, one launch (start us, length us, event | category | flops | bytes accessed | tf_op | source)
XLA Modules:
  0.0 295.4 jit_solution(428594510456169775)
XLA Ops:
  7.2 0.1 all-reduce.4.cloned.1.call-start
  7.2 1.7 slice.12
  9.0 5.7 %collective-permute-start = (s32[4,1024,128]{2,1,0:T(8,128)S(1)}, s32[4,1024,128]{2,1,0:T(8,128)S(1)}, u32[]{:S(2)}, u32[]{:S(2)}) collective-permute-start(s32[4,1024,128]{2,1,0:T(8,128)S(1)} %slice.12), channel_id=1, source_target_pairs={{0,1},{1,2},{2,3},{3,4},{4,5},{5,6},{6,7},{7,8},{8,9},{9,10},{10,1... | collective-permute-start | bytes 6291464 | tf_op jit(solution)/shard_map/ppermute | solution.py:356
  14.7 23.0 %collective-permute-done.halo_ref = s32[4,1024,128]{2,1,0:T(8,128)S(1)} collective-permute-done((s32[4,1024,128]{2,1,0:T(8,128)S(1)}, s32[4,1024,128]{2,1,0:T(8,128)S(1)}, u32[]{:S(2)}, u32[]{:S(2)}) %collective-permute-start) | collective-permute-done | bytes 2097184 | tf_op jit(solution)/shard_map/ppermute | solution.py:356
  37.7 0.0 copy-start.1
  37.7 1.3 copy-done.1
  39.0 0.0 copy-start
  39.0 35.7 %transform.1 = (f32[2,4,48,4096]{3,2,1,0:T(8,128)}, f32[12,32,128]{2,1,0:T(8,128)}) custom-call(s32[4,3072,128]{2,1,0:T(8,128)} %bitcast.17, s32[4,1024,128]{2,1,0:T(8,128)} %copy-done.1, f32[512,128]{1,0:T(8,128)} %bitcast.20, bf16[256,256]{1,0:T(8,128)(2,1)} %constant.12.clone.wh, bf16[256,256]{1,0:T(8,128)(2,1)} %constant.13.clone.wl, ...), custom_call_target="tpu_custom_call" | custom-call | flops 4000000000 | bytes 16000000 | tf_op jit(solution)/shard_map/transform/pallas_call | solution.py:265
  74.7 0.1 all-reduce.4.cloned.1.call-update
  74.8 0.1 all-reduce.6.cloned.1.call-start
  74.9 87.4 %all-reduce.4.cloned.1.call-done = f32[12,32,128]{2,1,0:T(8,128)} async-done(((f32[12,32,128]{2,1,0:T(8,128)}), f32[12,32,128]{2,1,0:T(8,128)}) %all-reduce.4.cloned.1.call-update) | async-done | bytes 196624 | tf_op jit(solution)/shard_map/psum | solution.py:365
  162.2 0.1 all-reduce.6.cloned.1.call-update
  162.3 0.1 all-reduce.8.cloned.1.call-start
  162.4 0.0 copy-done
  162.4 0.7 copy.10.pairs_ref
  163.0 76.2 %all-reduce.6.cloned.1.call-done = f32[12,32,128]{2,1,0:T(8,128)} async-done(((f32[12,32,128]{2,1,0:T(8,128)}), f32[12,32,128]{2,1,0:T(8,128)}) %all-reduce.6.cloned.1.call-update) | async-done | bytes 196624 | tf_op jit(solution)/shard_map/psum | solution.py:365
  239.2 0.1 all-reduce.8.cloned.1.call-update
  239.3 0.5 add_bitcast_fusion.canon_ref
  239.8 38.8 %all-reduce.8.cloned.1.call-done.sums_ref = f32[12,32,128]{2,1,0:T(8,128)} async-done(((f32[12,32,128]{2,1,0:T(8,128)}), f32[12,32,128]{2,1,0:T(8,128)}) %all-reduce.8.cloned.1.call-update) | async-done | bytes 196624 | tf_op jit(solution)/shard_map/psum | solution.py:365
  278.6 8.7 %normalize.1 = (f32[4,32,128]{2,1,0:T(8,128)}, f32[2,4,48,4096]{3,2,1,0:T(8,128)}) custom-call(s32[4]{0:T(128)} %add_bitcast_fusion.canon_ref, s32[4,2]{1,0:T(4,128)} %copy.10.pairs_ref, f32[12,32,128]{2,1,0:T(8,128)} %all-reduce.8.cloned.1.call-done.sums_ref, f32[2,4,48,4096]{3,2,1,0:T(8,128)} %get-tuple-element.7.prod_ref), custom_call_target="tpu_custom_call" | custom-call | flops 2000000 | bytes 13000000 | tf_op jit(solution)/shard_map/normalize/pallas_call | solution.py:317
  287.3 1.5 copy.13
Async XLA Ops:
  7.2 155.0 %all-reduce.4.cloned.1.call-start = ((), (), s32[]{:S(2)}) async-start(), calls=%async_computation | async-start | bytes 393216 | tf_op jit(solution)/shard_map/psum | solution.py:365
  9.0 28.7 %collective-permute-start = (s32[4,1024,128]{2,1,0:T(8,128)S(1)}, s32[4,1024,128]{2,1,0:T(8,128)S(1)}, u32[]{:S(2)}, u32[]{:S(2)}) collective-permute-start(s32[4,1024,128]{2,1,0:T(8,128)S(1)} %slice.12), channel_id=1, source_target_pairs={{0,1},{1,2},{2,3},{3,4},{4,5},{5,6},{6,7},{7,8},{8,9},{9,10},{10,1... | collective-permute-start | bytes 6291464 | tf_op jit(solution)/shard_map/ppermute | solution.py:356
  37.7 1.3 copy-start.1
  39.0 123.3 %copy-start = (s32[4,2]{0,1:T(2,128)S(1)}, s32[4,2]{0,1:T(2,128)}, u32[]{:S(2)}) copy-start(s32[4,2]{0,1:T(2,128)} %param.9) | copy-start | bytes 100
  74.8 164.4 %all-reduce.6.cloned.1.call-start = ((), (), s32[]{:S(2)}) async-start(), calls=%async_computation.1 | async-start | bytes 393216 | tf_op jit(solution)/shard_map/psum | solution.py:365
  162.3 116.3 %all-reduce.8.cloned.1.call-start = ((), (), s32[]{:S(2)}) async-start(), calls=%async_computation.2 | async-start | bytes 393216 | tf_op jit(solution)/shard_map/psum | solution.py:365
Sparse Core Ops, SparseCore 0:
  74.9 87.2 all-reduce.3
  164.6 74.6 all-reduce.5
  241.8 36.7 all-reduce.7
where the time goes:
time: 296 us; the launch traced here: 295 us
  waiting for transfers between devices  225 us (76%)
  Pallas kernels  44.4 us (15%)
  between operations  13.8 us (5%)
  starting transfers between devices  5.93 us (2%)
  local copies, waits for them, and re-layouts  5.23 us (2%)
    psum x3, waiting for transfers between devices, on_device(): sums = lax.psum(sums, axis)  202 us
    pallas_call x1, Pallas kernels, transform_call(): pl.pallas_call(transform_kernel, out_shape=(jax.ShapeDtypeStruct((2, 4, f...  35.7 us
    ppermute x1, waiting for transfers between devices, shifted(): return lax.ppermute(array, axis, pairs)  23 us
    pallas_call x1, Pallas kernels, normalize_call(): pl.pallas_call(functools.partial(normalize_kernel, total), grid_spec=pltp...  8.69 us
  transfers between devices with their start and end apart: 4, of which 4 were waited for; matrix products, arithmetic and copies ran while one was open for 0% of the time, Pallas kernels for 0%

commit v1 on v0

--- a/solution.py
+++ b/solution.py
@@ -117,25 +117,18 @@
     lax.fori_loop(0, 4, batch, 0)
 
 
-def permute_samples(raw, xf, frame0, row0, batches):
-    def batch(b, carry):
-        for c in range(2):
-            x = [raw[s, pl.ds((frame0 + 4 * b) * 64 + c, LANES, stride=2), :] for s in range(4)]
-            packed = (
-                (x[0] & 255)
-                | ((x[1] & 255) << 8)
-                | ((x[2] & 255) << 16)
-                | (x[3] << 24)
-            )
-            out = block_transpose(packed)
-            for q in range(4):
-                for s in range(4):
-                    value = out[q] << (24 - 8 * s) if s < 3 else out[q]
-                    value = (value >> 24).astype(jnp.float32)
-                    xf[2 * s + c, pl.ds(row0 + 4 * b + q, 32, stride=PITCH), :] = value
-        return carry
-
-    lax.fori_loop(0, batches, batch, 0)
+def permute_batch(raw, xf, b, row0):
+    for c in range(2):
+        x = [raw[s, pl.ds(b * 256 + c, LANES, stride=2), :] for s in range(4)]
+        packed = (
+            (x[0] & 255) | ((x[1] & 255) << 8) | ((x[2] & 255) << 16) | (x[3] << 24)
+        )
+        out = block_transpose(packed)
+        for q in range(4):
+            for s in range(4):
+                value = out[q] << (24 - 8 * s) if s < 3 else out[q]
+                value = (value >> 24).astype(jnp.float32)
+                xf[2 * s + c, pl.ds(row0 + 4 * b + q, 32, stride=PITCH), :] = value
 
 
 def process_group(group, refs):
@@ -182,7 +175,7 @@
                 at = pl.ds(pl.multiple_of(i * 32 + s * 8, 8), 8)
                 x = (v[at, :LANES], v[at, LANES:])
                 if i:
-                    c = twc[pl.ds(i, 8, stride=0), :] if False else jnp.broadcast_to(twc[i : i + 1, :], (8, LANES))
+                    c = jnp.broadcast_to(twc[i : i + 1, :], (8, LANES))
                     d = jnp.broadcast_to(tws[i : i + 1, :], (8, LANES))
                     x = (x[0] * c + x[1] * d, x[1] * c - x[0] * d)
                 xs.append(x)
@@ -224,53 +217,243 @@
     lax.fori_loop(0, 8, stage2b, 0)
 
 
+def peers():
+    x_name, y_name, c_name = TM
+    cores = lax.axis_size(c_name)
+    members = lax.axis_size(y_name) * cores
+    columns = lax.axis_size(x_name)
+    member = lax.axis_index(y_name) * cores + lax.axis_index(c_name)
+    return member, lax.axis_index(x_name), members, columns, cores
+
+
+def member_id(member, cores):
+    return {"tm_1": member // cores, "tm_2": lax.rem(member, cores)}
+
+
 def transform_kernel(
-    samples_ref, halo_ref, taps_ref, wh, wl, twc, tws, prod_ref, sums_ref,
-    xf, tapb, yh, yl, v, u, pbuf, sums, sems,
+    total, samples_ref, taps_ref, wh, wl, twc, tws, prod_ref, stats_ref,
+    raw, hraw, xf, tapb, yh, yl, v, u, pbuf, sums, part, rows_in, mine, cols_in, stat,
+    out_sems, in_sems, halo_send, halo_recv, row_send, row_recv, col_send, col_recv,
+    gat_send, gat_recv,
 ):
+    member, column, members, columns, cores = peers()
+    per = ROWS // members
+    count = members * columns
+    place = column * members + member
+    has_next = place < count - 1
+    has_prev = place > 0
+    MESH = pl.DeviceIdType.MESH
+
+    def tm_id(index):
+        return {"tm_0": index // members, **member_id(lax.rem(index, members), cores)}
+
+    def in_copy(b):
+        rows = pl.ds(pl.multiple_of(b * 256, 256), 256)
+        return pltpu.make_async_copy(samples_ref.at[:, rows, :], raw.at[:, rows, :], in_sems.at[b])
+
+    for b in range(12):
+        in_copy(b).start()
+
+    barrier = pltpu.get_barrier_semaphore()
+    for d in range(1, members):
+        other = lax.rem(member + d, members)
+        pl.semaphore_signal(
+            barrier, inc=1, device_id=member_id(other, cores), device_id_type=MESH
+        )
+    for d in range(1, columns):
+        other = lax.rem(column + d, columns)
+        pl.semaphore_signal(barrier, inc=1, device_id={"tm_0": other}, device_id_type=MESH)
+
+    first_member = member == 0
+    last_member = member == members - 1
+
+    @pl.when(jnp.logical_and(first_member, has_prev))
+    def _():
+        pl.semaphore_signal(barrier, inc=1, device_id=tm_id(place - 1), device_id_type=MESH)
+
+    greeted = members - 1 + columns - 1
+
+    @pl.when(jnp.logical_and(last_member, has_next))
+    def _():
+        pl.semaphore_wait(barrier, greeted + 1)
+
+    @pl.when(jnp.logical_not(jnp.logical_and(last_member, has_next)))
+    def _():
+        pl.semaphore_wait(barrier, greeted)
+
+    frames = samples_ref.shape[1] // 64
+
+    def halo_copy(b):
+        lead = 1 if b == 0 else 0
+        at = (4 * b + lead) * 64
+        size = (4 - lead) * 64
+        start = (frames - HALO) * 64 + at
+        return pltpu.make_async_remote_copy(
+            src_ref=samples_ref.at[:, pl.ds(start, size), :],
+            dst_ref=hraw.at[:, pl.ds(at, size), :],
+            send_sem=halo_send.at[b],
+            recv_sem=halo_recv.at[b],
+            device_id=tm_id(place + 1),
+            device_id_type=MESH,
+        )
+
+    @pl.when(has_next)
+    def _():
+        for b in (3, 2, 1, 0):
+            halo_copy(b).start()
+
+    @pl.when(jnp.logical_not(has_prev))
+    def _():
+        hraw[...] = jnp.zeros_like(hraw)
+
+    def halo_wait(b):
+        @pl.when(has_prev)
+        def _():
+            halo_copy(b).wait_recv()
+
     refs = (xf, tapb, wh, wl, twc, tws, yh, yl, v, u, pbuf, sums)
     sums[...] = jnp.zeros_like(sums)
     permute_taps(taps_ref, tapb)
-    permute_samples(samples_ref, xf, 0, HALO, 12)
-    permute_samples(halo_ref, xf, 0, 0, 4)
+
+    def own_batch(b, carry):
+        in_copy(b).wait()
+        permute_batch(raw, xf, b, HALO)
+        return carry
+
+    lax.fori_loop(0, 12, own_batch, 0)
 
     def out_copy(group):
         rows = pl.ds(pl.multiple_of(group * GROUP, 8), 8)
         return pltpu.make_async_copy(
-            pbuf.at[:, :, rows, :], prod_ref.at[:, :, rows, :], sems.at[group]
+            pbuf.at[:, :, rows, :], prod_ref.at[:, :, rows, :], out_sems.at[group]
         )
 
     def step(n, carry):
-        group = lax.rem(n + 2, 6)
+        group = n + 2 - (n // 4) * (2 * n - 3)
+
+        @pl.when(n == 4)
+        def _():
+            halo_wait(3)
+            halo_wait(2)
+            permute_batch(hraw, xf, 3, 0)
+            permute_batch(hraw, xf, 2, 0)
+
+        @pl.when(n == 5)
+        def _():
+            halo_wait(1)
+            halo_wait(0)
+            permute_batch(hraw, xf, 1, 0)
+            permute_batch(hraw, xf, 0, 0)
+
         process_group(group, refs)
         out_copy(group).start()
         return carry
 
     lax.fori_loop(0, 6, step, 0)
+
     for q in range(12):
         for k1 in range(ROWS):
-            sums_ref[q, k1 : k1 + 1, :] = jnp.sum(
+            at = q * per + k1 % per
+            part[k1 // per, at : at + 1, :] = jnp.sum(
                 sums[q, k1 * 8 : k1 * 8 + 8, :], axis=0, keepdims=True
             )
+
+    def row_copy(d):
+        other = lax.rem(member + d, members)
+        return pltpu.make_async_remote_copy(
+            src_ref=part.at[other],
+            dst_ref=rows_in.at[d - 1],
+            send_sem=row_send.at[d - 1],
+            recv_sem=row_recv.at[d - 1],
+            device_id=member_id(other, cores),
+            device_id_type=MESH,
+        )
+
+    for d in range(1, members):
+        row_copy(d).start()
+    acc = part[member]
+    for d in range(1, members):
+        row_copy(d).wait_recv()
+        acc = acc + rows_in[d - 1]
+    mine[...] = acc
+
+    def col_copy(d):
+        return pltpu.make_async_remote_copy(
+            src_ref=mine,
+            dst_ref=cols_in.at[d - 1],
+            send_sem=col_send.at[d - 1],
+            recv_sem=col_recv.at[d - 1],
+            device_id={"tm_0": lax.rem(column + d, columns)},
+            device_id_type=MESH,
+        )
+
+    for d in range(1, columns):
+        col_copy(d).start()
+    for d in range(1, columns):
+        col_copy(d).wait_recv()
+        acc = acc + cols_in[d - 1]
+    mean = acc * np.float32(1.0 / total)
+    power = [mean[per * s : per * (s + 1)] for s in range(4)]
+    coh = []
+    for p in range(4):
+        re = mean[per * (4 + p) : per * (5 + p)]
+        im = mean[per * (8 + p) : per * (9 + p)]
+        coh.append(
+            (re * re + im * im) / ((power[p // 2] + 1e-06) * (power[2 + p % 2] + 1e-06))
+        )
+    stat[...] = jnp.concatenate(power + coh, axis=0)
+    stats_ref[member] = stat[...]
+
+    def gather_copy(d):
+        return pltpu.make_async_remote_copy(
+            src_ref=stat,
+            dst_ref=stats_ref.at[member],
+            send_sem=gat_send.at[d - 1],
+            recv_sem=gat_recv.at[d - 1],
+            device_id=member_id(lax.rem(member + d, members), cores),
+            device_id_type=MESH,
+        )
+
+    for d in range(1, members):
+        gather_copy(d).start()
+    for d in range(1, members):
+        gather_copy(d).wait_recv()
+
+    @pl.when(has_next)
+    def _():
+        for b in range(4):
+            halo_copy(b).wait_send()
+
+    for d in range(1, members):
+        row_copy(d).wait_send()
+        gather_copy(d).wait_send()
+    for d in range(1, columns):
+        col_copy(d).wait_send()
     for group in range(6):
         out_copy(group).wait()
 
 
-def transform_call(rows, halo, taps_rows, interpret=False):
-    streams = rows.shape[0]
+def transform_call(rows, taps_rows, total):
     frames = rows.shape[1] // 64
     consts = [jnp.asarray(c) for c in constants()]
     vmem = pl.BlockSpec(memory_space=pltpu.VMEM)
-    f32, bf16 = jnp.float32, jnp.bfloat16
+    anywhere = pl.BlockSpec(memory_space=pl.ANY)
+    f32, bf16, i32 = jnp.float32, jnp.bfloat16, jnp.int32
+    members = lax.axis_size(TM[1]) * lax.axis_size(TM[2])
+    columns = lax.axis_size(TM[0])
+    per = ROWS // members
+    dma = pltpu.SemaphoreType.DMA
     return pl.pallas_call(
-        transform_kernel,
+        functools.partial(transform_kernel, total),
         out_shape=(
             jax.ShapeDtypeStruct((2, 4, frames, 4096), f32),
-            jax.ShapeDtypeStruct((12, ROWS, LANES), f32),
+            jax.ShapeDtypeStruct((members, 8 * per, LANES), f32),
         ),
-        in_specs=[vmem] * 7,
-        out_specs=(pl.BlockSpec(memory_space=pl.ANY), vmem),
+        in_specs=[anywhere] + [vmem] * 5,
+        out_specs=(anywhere, vmem),
         scratch_shapes=[
+            pltpu.VMEM((4, frames * 64, LANES), i32),
+            pltpu.VMEM((4, HALO * 64, LANES), i32),
             pltpu.VMEM((8, ROWS * PITCH + 7, LANES), f32),
             pltpu.VMEM((ROWS * 16 * 8, LANES), f32),
             pltpu.VMEM((1024, 256), bf16),
@@ -279,48 +462,68 @@
             pltpu.VMEM((2, 1024, LANES), f32),
             pltpu.VMEM((2, 4, frames, 4096), f32),
             pltpu.VMEM((12, ROWS * 8, LANES), f32),
-            pltpu.SemaphoreType.DMA((6,)),
+            pltpu.VMEM((members, 12 * per, LANES), f32),
+            pltpu.VMEM((members - 1, 12 * per, LANES), f32),
+            pltpu.VMEM((12 * per, LANES), f32),
+            pltpu.VMEM((columns - 1, 12 * per, LANES), f32),
+            pltpu.VMEM((8 * per, LANES), f32),
+            dma((6,)),
+            dma((12,)),
+            dma((4,)),
+            dma((4,)),
+            dma((members - 1,)),
+            dma((members - 1,)),
+            dma((columns - 1,)),
+            dma((columns - 1,)),
+            dma((members - 1,)),
+            dma((members - 1,)),
         ],
-        compiler_params=pltpu.CompilerParams(vmem_limit_bytes=60 * 1024 * 1024),
-        cost_estimate=pl.CostEstimate(flops=4_000_000_000, bytes_accessed=16_000_000, transcendentals=0),
-        interpret=interpret,
+        compiler_params=pltpu.CompilerParams(
+            vmem_limit_bytes=60 * 1024 * 1024, collective_id=0, has_side_effects=True
+        ),
+        cost_estimate=pl.CostEstimate(
+            flops=4_000_000_000, bytes_accessed=16_000_000, transcendentals=0
+        ),
         name="transform",
-    )(rows, halo, taps_rows, *consts)
-
-
-def normalize_kernel(total, canon_ref, pairs_ref, sums_ref, prod_ref, coh_ref, out_ref):
+    )(rows, taps_rows, *consts)
+
+
+def normalize_kernel(canon_ref, pairs_ref, stats_ref, prod_ref, coh_ref, out_ref):
     pair = pl.program_id(0)
     canon = canon_ref[pair]
     first = pairs_ref[pair, 0]
     second = pairs_ref[pair, 1]
-    scale = np.float32(1.0 / total)
-    power = (sums_ref[first] * scale + 1e-06) * (sums_ref[second] * scale + 1e-06)
-    factor = 1.0 / jnp.sqrt(power)
+    members = stats_ref.shape[0]
+    per = ROWS // members
+    for m in range(members):
+        power = (stats_ref[m, pl.ds(first * per, per), :] + 1e-06) * (
+            stats_ref[m, pl.ds(second * per, per), :] + 1e-06
+        )
+        factor = 1.0 / jnp.sqrt(power)
+        for r in range(per):
+            k1 = m * per + r
+            cols = slice(k1 * LANES, (k1 + 1) * LANES)
+            row = factor[r : r + 1]
+            for part in range(2):
+                out_ref[part, 0, :, cols] = prod_ref[part, 0, :, cols] * row
 
     @pl.when(pl.program_id(1) == 0)
     def _():
-        re = sums_ref[4 + canon] * scale
-        im = sums_ref[8 + canon] * scale
-        coh_ref[0] = (re * re + im * im) / power
-
-    for k1 in range(ROWS):
-        cols = slice(k1 * LANES, (k1 + 1) * LANES)
-        row = factor[k1 : k1 + 1]
-        for part in range(2):
-            out_ref[part, 0, :, cols] = prod_ref[part, 0, :, cols] * row
-
-
-def normalize_call(pairs, sums, prods, total, block=24, interpret=False):
+        for m in range(members):
+            coh_ref[0, m * per : (m + 1) * per, :] = stats_ref[m, pl.ds((4 + canon) * per, per), :]
+
+
+def normalize_call(pairs, stats, prods, block=24):
     frames = prods.shape[2]
     canon = pairs[:, 0] * 2 + pairs[:, 1] - 2
     f32 = jnp.float32
     coh, normalized = pl.pallas_call(
-        functools.partial(normalize_kernel, total),
+        normalize_kernel,
         grid_spec=pltpu.PrefetchScalarGridSpec(
             num_scalar_prefetch=2,
             grid=(4, frames // block),
             in_specs=[
-                pl.BlockSpec((12, ROWS, LANES), lambda p, b, canon, pairs: (0, 0, 0)),
+                pl.BlockSpec(stats.shape, lambda p, b, canon, pairs: (0, 0, 0)),
                 pl.BlockSpec((2, 1, block, 4096), lambda p, b, canon, pairs: (0, canon[p], b, 0)),
             ],
             out_specs=[
@@ -333,9 +536,8 @@
             jax.ShapeDtypeStruct(prods.shape, f32),
         ),
         cost_estimate=pl.CostEstimate(flops=2_000_000, bytes_accessed=13_000_000, transcendentals=0),
-        interpret=interpret,
         name="normalize",
-    )(canon, pairs, sums, prods)
+    )(canon, pairs, stats, prods)
     return coh.reshape(4, ROWS * LANES), normalized
 
 
@@ -350,21 +552,11 @@
     return jnp.transpose(taps, (0, 2, 1, 3)).reshape(512, LANES)
 
 
-def shifted(array, axis, by):
-    devices = lax.axis_size(axis)
-    pairs = [(i, i + by) for i in range(devices) if 0 <= i + by < devices]
-    return lax.ppermute(array, axis, pairs)
-
-
 def on_device(volts, taps, pairs):
     rows = sample_rows(volts)
-    frames = rows.shape[1] // 64
-    halo = shifted(rows[:, (frames - HALO) * 64 :], TM, 1)
-    prods, sums = transform_call(rows, halo, tap_rows(taps))
-    for axis in TM:
-        sums = lax.psum(sums, axis)
-    total = frames * lax.axis_size(TM)
-    return normalize_call(pairs, sums, prods, total)
+    total = rows.shape[1] // 64 * lax.axis_size(TM)
+    prods, stats = transform_call(rows, tap_rows(taps), total)
+    return normalize_call(pairs, stats, prods)
 
 
 def solution(mesh):

time: 296 us -> 88.4 us (0.30)
  waiting for transfers between devices: 225 us -> 0 us
  Pallas kernels: 44.4 us -> 83.2 us
  between operations: 13.8 us -> 0.64 us
  starting transfers between devices: 5.93 us -> 0 us
    psum x3 -> x0, waiting for transfers between devices: 202 us -> none  [on_device(): sums = lax.psum(sums, axis)]
    pallas_call x2, Pallas kernels: 44.4 us -> 83.2 us  [the longest x1 74.4 us: transform_call(): pl.pallas_call(functools.partial(transform_kernel, total), out_shape=(jax...]
    ppermute x1 -> x0, waiting for transfers between devices: 23 us -> none  [shifted(): return lax.ppermute(array, axis, pairs)]
    ppermute x1 -> x0, starting transfers between devices: 5.75 us -> none  [shifted(): return lax.ppermute(array, axis, pairs)]
  transfers between devices with their start and end apart: 4 -> 0, of which waited for: 4 -> 0; matrix products, arithmetic and copies ran while one was open for 0% -> 0% of each run, Pallas kernels for 0% -> 0%
where the time goes in v1:
time: 88.4 us; the launch traced here: 88 us
  Pallas kernels  83.2 us (94%)
  local copies, waits for them, and re-layouts  2.85 us (3%)
  other arithmetic  1.35 us (2%)
    pallas_call x1, Pallas kernels, transform_call(): pl.pallas_call(functools.partial(transform_kernel, total), out_shape=(jax...  74.4 us
    pallas_call x1, Pallas kernels, normalize_call(): pl.pallas_call(normalize_kernel, grid_spec=pltpu.PrefetchScalarGridSpec(n...  8.7 us
    unnamed x2, local copies, waits for them, and re-layouts  2.85 us

profile of v1, /device:TPU:513, one launch (start us, length us, event | category | flops | bytes accessed | tf_op | source)
XLA Modules:
  0.0 88.0 jit_solution(5385407333125660636)
XLA Ops:
  0.6 1.3 %add_bitcast_fusion.canon_ref = s32[4]{0:T(128)} fusion(s32[4,2]{0,1:T(2,128)} %param.9), kind=kLoop, calls=%fused_computation.1 | loop fusion | flops 12 | bytes 48 | tf_op jit(solution)/shard_map/sub | solution.py:518
  2.0 1.3 %copy.10.pairs_ref = s32[4,2]{1,0:T(4,128)} copy(s32[4,2]{0,1:T(2,128)} %param.9) | data formatting | bytes 64 | tf_op args[2]
  3.3 74.4 %transform.1 = (f32[2,4,48,4096]{3,2,1,0:T(8,128)}, f32[16,16,128]{2,1,0:T(8,128)}) custom-call(s32[4,3072,128]{2,1,0:T(8,128)} %bitcast.18, f32[512,128]{1,0:T(8,128)} %bitcast.19, bf16[256,256]{1,0:T(8,128)(2,1)} %constant.12.clone.wh, bf16[256,256]{1,0:T(8,128)(2,1)} %constant.13.clone.wl, f32[32,128]{1,0:T(8,128)} %constant.14.clone.twc, ...), custom_call_target="tpu_custom_call" | custom-call | flops 4000000000 | bytes 16000000 | tf_op jit(solution)/shard_map/transform/pallas_call | solution.py:446
  77.8 8.7 %normalize.1 = (f32[4,32,128]{2,1,0:T(8,128)}, f32[2,4,48,4096]{3,2,1,0:T(8,128)}) custom-call(s32[4]{0:T(128)} %add_bitcast_fusion.canon_ref, s32[4,2]{1,0:T(4,128)} %copy.10.pairs_ref, f32[16,16,128]{2,1,0:T(8,128)} %get-tuple-element.6.stats_ref, f32[2,4,48,4096]{3,2,1,0:T(8,128)} %get-tuple-element.7.prod_ref), custom_call_target="tpu_custom_call" | custom-call | flops 2000000 | bytes 13000000 | tf_op jit(solution)/shard_map/normalize/pallas_call | solution.py:520
  86.5 1.5 %copy.13 = f32[1,4,32,128]{3,1,2,0:T(4,128)} copy(f32[1,4,32,128]{3,2,1,0:T(8,128)} %bitcast.16) | data formatting | bytes 131072

commit v2 on v1

--- a/solution.py
+++ b/solution.py
@@ -131,48 +131,65 @@
                 xf[2 * s + c, pl.ds(row0 + 4 * b + q, 32, stride=PITCH), :] = value
 
 
-def process_group(group, refs):
-    (xf, tapb, wh, wl, twc, tws, yh, yl, v, u, pbuf, sums) = refs
-
-    def fir(i, carry):
-        base = i * PITCH + HALO + group * GROUP
-        tap = [
-            tapb[pl.ds(pl.multiple_of((i * 16 + t) * 8, 8), 8), :] for t in range(16)
-        ]
+def order_of(i):
+    return lax.rem(i, 4) * 8 + i // 4
+
+
+def fir(refs, first, groups, tap0, tap1, extend=False):
+    (xf, tapb, y) = refs
+
+    def body(i, carry):
+        base = i * PITCH + HALO + first * GROUP
+        place = order_of(i)
+        tap = {
+            t: tapb[pl.ds(pl.multiple_of((i * 16 + t) * 8, 8), 8), :] for t in range(tap0, tap1)
+        }
         for c in range(2):
-            for pair in range(2):
-                ys = []
-                for s in (2 * pair, 2 * pair + 1):
-                    acc = None
-                    for t in range(16):
-                        term = tap[t] * xf[2 * s + c, pl.ds(base - t, 8), :]
-                        acc = term if acc is None else acc + term
-                    ys.append(acc)
-                y = jnp.concatenate(ys, axis=0)
-                high = y.astype(jnp.bfloat16)
-                low = (y - high.astype(jnp.float32)).astype(jnp.bfloat16)
-                at = pl.ds(pl.multiple_of(i * 32 + pair * 16, 16), 16)
-                yh[at, c * LANES : (c + 1) * LANES] = high
-                yl[at, c * LANES : (c + 1) * LANES] = low
+            cols = slice(c * LANES, (c + 1) * LANES)
+            for s in range(4):
+                at = [
+                    pl.ds(pl.multiple_of((g * 128 + s * 32 + place) * 8, 8), 8)
+                    for g in range(groups)
+                ]
+                acc = [y[at[g], cols] if extend else None for g in range(groups)]
+                for w in range(1 - tap1, 8 * (groups - 1) - tap0 + 1):
+                    users = [g for g in range(groups) if tap0 <= 8 * g - w < tap1]
+                    if not users:
+                        continue
+                    x = xf[2 * s + c, pl.ds(base + w, 8), :]
+                    for g in users:
+                        term = tap[8 * g - w] * x
+                        acc[g] = term if acc[g] is None else acc[g] + term
+                for g in range(groups):
+                    y[at[g], cols] = acc[g]
         return carry
 
-    lax.fori_loop(0, ROWS, fir, 0)
+    lax.fori_loop(0, ROWS, body, 0)
+
+
+def transform(refs, group0, groups):
+    (y, wh, wl, twc, tws, v, u, pbuf, sums) = refs
 
     def stage1(m, carry):
-        at = pl.ds(pl.multiple_of(m * 256, 256), 256)
-        h, l = yh[at, :], yl[at, :]
+        at = pl.ds(pl.multiple_of(m * 512, 512), 512)
+        x = y[at, :]
+        h = x.astype(jnp.bfloat16)
+        l = (x - h.astype(jnp.float32)).astype(jnp.bfloat16)
         dot = functools.partial(jnp.dot, preferred_element_type=jnp.float32)
         v[at, :] = dot(h, wh[...]) + dot(l, wh[...]) + dot(h, wl[...])
         return carry
 
-    lax.fori_loop(0, 4, stage1, 0)
-
-    def stage2a(s, carry):
+    lax.fori_loop(0, 2 * groups, stage1, 0)
+
+    def tile(n):
+        return pl.ds(pl.multiple_of(n * 8, 8), 8)
+
+    def stage2a(gs, carry):
         for i0 in range(4):
             xs = []
             for i1 in range(8):
                 i = 4 * i1 + i0
-                at = pl.ds(pl.multiple_of(i * 32 + s * 8, 8), 8)
+                at = tile(gs * 32 + i0 * 8 + i1)
                 x = (v[at, :LANES], v[at, LANES:])
                 if i:
                     c = jnp.broadcast_to(twc[i : i + 1, :], (8, LANES))
@@ -181,28 +198,30 @@
                 xs.append(x)
             for ka, x in enumerate(fft8(xs)):
                 x = rotate(x, i0 * ka, 32)
-                at = pl.ds(pl.multiple_of((s * 32 + i0 * 8 + ka) * 8, 8), 8)
+                at = tile(gs * 37 + i0 * 9 + ka)
                 u[0, at, :] = x[0]
                 u[1, at, :] = x[1]
         return carry
 
-    lax.fori_loop(0, 4, stage2a, 0)
-
-    def stage2b(ka, carry):
+    lax.fori_loop(0, 4 * groups, stage2a, 0)
+
+    def stage2b(n, carry):
+        g = n // 8
+        ka = lax.rem(n, 8)
+        rows = tile(group0 + g)
         spectra = []
         for s in range(4):
             xs = []
             for i0 in range(4):
-                at = pl.ds(pl.multiple_of((s * 32 + i0 * 8 + ka) * 8, 8), 8)
+                at = tile((g * 4 + s) * 37 + i0 * 9 + ka)
                 xs.append((u[0, at, :], u[1, at, :]))
             spectra.append(fft4(xs))
         for kb in range(4):
             k1 = ka + 8 * kb
             z = [spectra[s][kb] for s in range(4)]
-            at = pl.ds(pl.multiple_of(k1 * 8, 8), 8)
+            at = tile(k1)
             for s in range(4):
                 sums[s, at, :] += z[s][0] * z[s][0] + z[s][1] * z[s][1]
-            rows = pl.ds(pl.multiple_of(group * GROUP, 8), 8)
             cols = pl.ds(pl.multiple_of(k1 * LANES, LANES), LANES)
             for p in range(4):
                 a, b = z[p // 2], z[2 + p % 2]
@@ -214,7 +233,7 @@
                 pbuf[1, p, rows, cols] = im
         return carry
 
-    lax.fori_loop(0, 8, stage2b, 0)
+    lax.fori_loop(0, 8 * groups, stage2b, 0)
 
 
 def peers():
@@ -232,7 +251,7 @@
 
 def transform_kernel(
     total, samples_ref, taps_ref, wh, wl, twc, tws, prod_ref, stats_ref,
-    raw, hraw, xf, tapb, yh, yl, v, u, pbuf, sums, part, rows_in, mine, cols_in, stat,
+    raw, hraw, xf, tapb, y, v, u, pbuf, sums, part, rows_in, mine, cols_in, stat,
     out_sems, in_sems, halo_send, halo_recv, row_send, row_recv, col_send, col_recv,
     gat_send, gat_recv,
 ):
@@ -311,7 +330,8 @@
         def _():
             halo_copy(b).wait_recv()
 
-    refs = (xf, tapb, wh, wl, twc, tws, yh, yl, v, u, pbuf, sums)
+    filters = (xf, tapb, y)
+    refs = (y, wh, wl, twc, tws, v, u, pbuf, sums)
     sums[...] = jnp.zeros_like(sums)
     permute_taps(taps_ref, tapb)
 
@@ -322,34 +342,32 @@
 
     lax.fori_loop(0, 12, own_batch, 0)
 
-    def out_copy(group):
-        rows = pl.ds(pl.multiple_of(group * GROUP, 8), 8)
+    def out_copy(n):
+        rows = (pl.ds(0, 8), pl.ds(8, 8), pl.ds(16, frames - 16))[n]
         return pltpu.make_async_copy(
-            pbuf.at[:, :, rows, :], prod_ref.at[:, :, rows, :], out_sems.at[group]
-        )
-
-    def step(n, carry):
-        group = n + 2 - (n // 4) * (2 * n - 3)
-
-        @pl.when(n == 4)
-        def _():
-            halo_wait(3)
-            halo_wait(2)
-            permute_batch(hraw, xf, 3, 0)
-            permute_batch(hraw, xf, 2, 0)
-
-        @pl.when(n == 5)
-        def _():
-            halo_wait(1)
-            halo_wait(0)
-            permute_batch(hraw, xf, 1, 0)
-            permute_batch(hraw, xf, 0, 0)
-
-        process_group(group, refs)
-        out_copy(group).start()
-        return carry
-
-    lax.fori_loop(0, 6, step, 0)
+            pbuf.at[:, :, rows, pl.ds(0, 4096)], prod_ref.at[:, :, rows, :], out_sems.at[n]
+        )
+
+    fir(filters, 2, 4, 0, 16)
+    transform(refs, 2, 4)
+    out_copy(2).start()
+
+    halo_wait(3)
+    halo_wait(2)
+    permute_batch(hraw, xf, 3, 0)
+    permute_batch(hraw, xf, 2, 0)
+    fir(filters, 1, 1, 0, 16)
+    transform(refs, 1, 1)
+    out_copy(1).start()
+
+    halo_wait(1)
+    permute_batch(hraw, xf, 1, 0)
+    fir(filters, 0, 1, 0, 13)
+    halo_wait(0)
+    permute_batch(hraw, xf, 0, 0)
+    fir(filters, 0, 1, 13, 16, extend=True)
+    transform(refs, 0, 1)
+    out_copy(0).start()
 
     for q in range(12):
         for k1 in range(ROWS):
@@ -429,8 +447,8 @@
         gather_copy(d).wait_send()
     for d in range(1, columns):
         col_copy(d).wait_send()
-    for group in range(6):
-        out_copy(group).wait()
+    for n in range(3):
+        out_copy(n).wait()
 
 
 def transform_call(rows, taps_rows, total):
@@ -438,7 +456,7 @@
     consts = [jnp.asarray(c) for c in constants()]
     vmem = pl.BlockSpec(memory_space=pltpu.VMEM)
     anywhere = pl.BlockSpec(memory_space=pl.ANY)
-    f32, bf16, i32 = jnp.float32, jnp.bfloat16, jnp.int32
+    f32, i32 = jnp.float32, jnp.int32
     members = lax.axis_size(TM[1]) * lax.axis_size(TM[2])
     columns = lax.axis_size(TM[0])
     per = ROWS // members
@@ -456,18 +474,17 @@
             pltpu.VMEM((4, HALO * 64, LANES), i32),
             pltpu.VMEM((8, ROWS * PITCH + 7, LANES), f32),
             pltpu.VMEM((ROWS * 16 * 8, LANES), f32),
-            pltpu.VMEM((1024, 256), bf16),
-            pltpu.VMEM((1024, 256), bf16),
-            pltpu.VMEM((1024, 256), f32),
-            pltpu.VMEM((2, 1024, LANES), f32),
-            pltpu.VMEM((2, 4, frames, 4096), f32),
-            pltpu.VMEM((12, ROWS * 8, LANES), f32),
+            pltpu.VMEM((4096, 256), f32),
+            pltpu.VMEM((4096, 256), f32),
+            pltpu.VMEM((2, 16 * 37 * 8 + 16, LANES), f32),
+            pltpu.VMEM((2, 4, frames, 4096 + LANES), f32),
+            pltpu.VMEM((12, (ROWS + 1) * 8, LANES), f32),
             pltpu.VMEM((members, 12 * per, LANES), f32),
             pltpu.VMEM((members - 1, 12 * per, LANES), f32),
             pltpu.VMEM((12 * per, LANES), f32),
             pltpu.VMEM((columns - 1, 12 * per, LANES), f32),
             pltpu.VMEM((8 * per, LANES), f32),
-            dma((6,)),
+            dma((3,)),
             dma((12,)),
             dma((4,)),
             dma((4,)),
@@ -488,57 +505,65 @@
     )(rows, taps_rows, *consts)
 
 
-def normalize_kernel(canon_ref, pairs_ref, stats_ref, prod_ref, coh_ref, out_ref):
+def normalize_kernel(stats_per, pairs_ref, stats_ref, prod_ref, coh_ref, out_ref):
     pair = pl.program_id(0)
-    canon = canon_ref[pair]
-    first = pairs_ref[pair, 0]
-    second = pairs_ref[pair, 1]
-    members = stats_ref.shape[0]
-    per = ROWS // members
-    for m in range(members):
-        power = (stats_ref[m, pl.ds(first * per, per), :] + 1e-06) * (
-            stats_ref[m, pl.ds(second * per, per), :] + 1e-06
-        )
+    first = pairs_ref[0, pair]
+    second = pairs_ref[1, pair]
+    per = stats_per
+    members = ROWS // per
+
+    def stat(q, r):
+        return stats_ref[pl.ds(q * per + r, members, stride=8 * per), :]
+
+    for r in range(per):
+        power = (stat(first, r) + 1e-06) * (stat(second, r) + 1e-06)
         factor = 1.0 / jnp.sqrt(power)
-        for r in range(per):
+        for m in range(members):
             k1 = m * per + r
             cols = slice(k1 * LANES, (k1 + 1) * LANES)
-            row = factor[r : r + 1]
+            row = factor[m : m + 1]
             for part in range(2):
                 out_ref[part, 0, :, cols] = prod_ref[part, 0, :, cols] * row
 
-    @pl.when(pl.program_id(1) == 0)
-    def _():
-        for m in range(members):
-            coh_ref[0, m * per : (m + 1) * per, :] = stats_ref[m, pl.ds((4 + canon) * per, per), :]
+    @pl.when(jnp.logical_and(pair == 0, pl.program_id(1) == 0))
+    def _():
+        for p in range(4):
+            which = pairs_ref[0, p] * 2 + pairs_ref[1, p] - 2
+            for r in range(per):
+                value = stat(4 + which, r)
+                for m in range(members):
+                    k1 = m * per + r
+                    coh_ref[p : p + 1, k1 * LANES : (k1 + 1) * LANES] = value[m : m + 1]
 
 
 def normalize_call(pairs, stats, prods, block=24):
     frames = prods.shape[2]
-    canon = pairs[:, 0] * 2 + pairs[:, 1] - 2
     f32 = jnp.float32
-    coh, normalized = pl.pallas_call(
-        normalize_kernel,
+    table = stats.reshape(-1, LANES)
+    return pl.pallas_call(
+        functools.partial(normalize_kernel, stats.shape[1] // 8),
         grid_spec=pltpu.PrefetchScalarGridSpec(
-            num_scalar_prefetch=2,
+            num_scalar_prefetch=1,
             grid=(4, frames // block),
             in_specs=[
-                pl.BlockSpec(stats.shape, lambda p, b, canon, pairs: (0, 0, 0)),
-                pl.BlockSpec((2, 1, block, 4096), lambda p, b, canon, pairs: (0, canon[p], b, 0)),
+                pl.BlockSpec(table.shape, lambda p, b, pairs: (0, 0)),
+                pl.BlockSpec(
+                    (2, 1, block, 4096),
+                    lambda p, b, pairs: (0, pairs[0, p] * 2 + pairs[1, p] - 2, b, 0),
+                ),
             ],
             out_specs=[
-                pl.BlockSpec((1, ROWS, LANES), lambda p, b, canon, pairs: (p, 0, 0)),
-                pl.BlockSpec((2, 1, block, 4096), lambda p, b, canon, pairs: (0, p, b, 0)),
+                pl.BlockSpec((4, 4096), lambda p, b, pairs: (0, 0)),
+                pl.BlockSpec((2, 1, block, 4096), lambda p, b, pairs: (0, p, b, 0)),
             ],
         ),
         out_shape=(
-            jax.ShapeDtypeStruct((4, ROWS, LANES), f32),
+            jax.ShapeDtypeStruct((4, 4096), f32),
             jax.ShapeDtypeStruct(prods.shape, f32),
         ),
         cost_estimate=pl.CostEstimate(flops=2_000_000, bytes_accessed=13_000_000, transcendentals=0),
         name="normalize",
-    )(canon, pairs, stats, prods)
-    return coh.reshape(4, ROWS * LANES), normalized
+    )(pairs.T, table, prods)
 
 
 def sample_rows(volts):

time: 88.4 us -> 79.3 us (0.90)
  Pallas kernels: 83.2 us -> 78.4 us
  local copies, waits for them, and re-layouts: 2.85 us -> 0 us
  other arithmetic: 1.35 us -> 0 us
    pallas_call x1, Pallas kernels: 74.4 us -> 69.5 us  [transform_call(): pl.pallas_call(functools.partial(transform_kernel, total), out_shape=(jax...]
    unnamed x2 -> x0, local copies, waits for them, and re-layouts: 2.85 us -> none
    sub x1 -> x0, other arithmetic: 1.35 us -> none  [normalize_call(): canon = pairs[:, 0] * 2 + pairs[:, 1] - 2]
where the time goes in v2:
time: 79.3 us; the launch traced here: 79 us
  Pallas kernels  78.4 us (99%)
    pallas_call x1, Pallas kernels, transform_call(): pl.pallas_call(functools.partial(transform_kernel, total), out_shape=(jax...  69.5 us
    pallas_call x1, Pallas kernels, normalize_call(): pl.pallas_call(functools.partial(normalize_kernel, stats.shape[1] // 8),...  8.81 us

profile of v2, /device:TPU:513, one launch (start us, length us, event | category | flops | bytes accessed | tf_op | source)
XLA Modules:
  0.0 79.0 jit_solution(4889131528424129843)
XLA Ops:
  0.6 69.5 %transform.1 = (f32[2,4,48,4096]{3,2,1,0:T(8,128)}, f32[16,16,128]{2,1,0:T(8,128)}) custom-call(s32[4,3072,128]{2,1,0:T(8,128)} %bitcast.14, f32[512,128]{1,0:T(8,128)} %bitcast.15, bf16[256,256]{1,0:T(8,128)(2,1)} %constant.8.clone.wh, bf16[256,256]{1,0:T(8,128)(2,1)} %constant.9.clone.wl, f32[32,128]{1,0:T(8,128)} %constant.10.clone.twc, ...), custom_call_target="tpu_custom_call" | custom-call | flops 4000000000 | bytes 16000000 | tf_op jit(solution)/shard_map/transform/pallas_call | solution.py:464
  70.2 8.8 %normalize.1 = (f32[4,4096]{1,0:T(4,128)}, f32[2,4,48,4096]{3,2,1,0:T(8,128)}) custom-call(s32[2,4]{1,0:T(2,128)} %bitcast.13, f32[256,128]{1,0:T(8,128)} %bitcast.12, f32[2,4,48,4096]{3,2,1,0:T(8,128)} %get-tuple-element.5.prod_ref), custom_call_target="tpu_custom_call" | custom-call | flops 2000000 | bytes 13000000 | tf_op jit(solution)/shard_map/normalize/pallas_call | solution.py:543

commit v3 on v2

--- a/solution.py
+++ b/solution.py
@@ -236,35 +236,176 @@
     lax.fori_loop(0, 8 * groups, stage2b, 0)
 
 
-def peers():
-    x_name, y_name, c_name = TM
-    cores = lax.axis_size(c_name)
-    members = lax.axis_size(y_name) * cores
-    columns = lax.axis_size(x_name)
-    member = lax.axis_index(y_name) * cores + lax.axis_index(c_name)
-    return member, lax.axis_index(x_name), members, columns, cores
-
-
-def member_id(member, cores):
-    return {"tm_1": member // cores, "tm_2": lax.rem(member, cores)}
+HALF = ROWS // 2
+
+
+class Ring:
+    def __init__(self, half, a, b):
+        self.half, self.a, self.b, self.c = half, a, b, TM[2]
+        self.na, self.nb, self.nc = (lax.axis_size(n) for n in (a, b, self.c))
+        self.members = self.na * self.nc
+        self.per = HALF // self.members
+        far = sorted(range(self.na), key=lambda d: -min(d, self.na - d))
+        self.steps = [(d, e) for d in far for e in range(self.nc) if (d, e) != (0, 0)]
+        self.shifts = sorted(range(1, self.nb), key=lambda d: -min(d, self.nb - d))
+
+    def member(self, d=0, e=0):
+        at = lax.rem(lax.axis_index(self.a) + d, self.na)
+        core = lax.rem(lax.axis_index(self.c) + e, self.nc)
+        return at * self.nc + core
+
+    def member_id(self, d, e):
+        return {
+            self.a: lax.rem(lax.axis_index(self.a) + d, self.na),
+            self.c: lax.rem(lax.axis_index(self.c) + e, self.nc),
+        }
+
+    def column_id(self, d):
+        return {self.b: lax.rem(lax.axis_index(self.b) + d, self.nb)}
+
+
+def rings():
+    return (Ring(0, TM[1], TM[0]), Ring(1, TM[0], TM[1]))
+
+
+def remote(src, dst, send, recv, to):
+    return pltpu.make_async_remote_copy(
+        src_ref=src,
+        dst_ref=dst,
+        send_sem=send,
+        recv_sem=recv,
+        device_id=to,
+        device_id_type=pl.DeviceIdType.MESH,
+    )
+
+
+def all_reduce(total, sums, stats_ref, scratch):
+    both = rings()
+    work = []
+    for ring in both:
+        part, rows_in, mine, cols_in, stat, sems = scratch[ring.half]
+        work.append((ring, part, rows_in, mine, cols_in, stat, sems))
+
+    def row_copy(job, n):
+        ring, part, rows_in, _, _, _, sems = job
+        d, e = ring.steps[n]
+        return remote(
+            part.at[ring.member(d, e)], rows_in.at[n], sems.at[0, n], sems.at[1, n],
+            ring.member_id(d, e),
+        )
+
+    def col_copy(job, n):
+        ring, _, _, mine, cols_in, _, sems = job
+        return remote(
+            mine, cols_in.at[n], sems.at[2, n], sems.at[3, n], ring.column_id(ring.shifts[n])
+        )
+
+    def place(ring):
+        return pl.ds(HALF * ring.half + ring.member() * ring.per, ring.per)
+
+    def gather_copy(job, n):
+        ring, _, _, _, _, stat, sems = job
+        return remote(
+            stat, stats_ref.at[place(ring)], sems.at[4, n], sems.at[5, n],
+            ring.member_id(*ring.steps[n]),
+        )
+
+    for job in work:
+        ring, part = job[:2]
+        for k in range(HALF):
+            k1 = HALF * ring.half + k
+            for j in range(3):
+                part[k // ring.per, k % ring.per, j] = jnp.concatenate(
+                    [
+                        jnp.sum(sums[4 * j + q, k1 * 8 : k1 * 8 + 8, :], axis=0, keepdims=True)
+                        for q in range(4)
+                    ],
+                    axis=0,
+                )
+        for n in range(len(ring.steps)):
+            row_copy(job, n).start()
+
+    totals = []
+    for job in work:
+        ring, part, rows_in, mine = job[:4]
+        acc = part[ring.member()]
+        for n in reversed(range(len(ring.steps))):
+            row_copy(job, n).wait_recv()
+            acc = acc + rows_in[n]
+        mine[...] = acc
+        for n in range(len(ring.shifts)):
+            col_copy(job, n).start()
+        totals.append(acc)
+
+    for job, acc in zip(work, totals):
+        ring, _, _, _, cols_in, stat, _ = job
+        for n in reversed(range(len(ring.shifts))):
+            col_copy(job, n).wait_recv()
+            acc = acc + cols_in[n]
+        mean = acc * np.float32(1.0 / total)
+        for r in range(ring.per):
+            power, re, im = mean[r, 0], mean[r, 1], mean[r, 2]
+            raised = power + 1e-06
+            denom = jnp.concatenate(
+                [raised[p // 2 : p // 2 + 1] * raised[2 + p % 2 : 3 + p % 2] for p in range(4)],
+                axis=0,
+            )
+            stat[r, 0] = power
+            stat[r, 1] = (re * re + im * im) / denom
+        for n in range(len(ring.steps)):
+            gather_copy(job, n).start()
+        stats_ref[place(ring)] = stat[...]
+
+    for job in work:
+        ring = job[0]
+        for n in reversed(range(len(ring.steps))):
+            gather_copy(job, n).wait_recv()
+    for job in work:
+        ring = job[0]
+        for n in range(len(ring.steps)):
+            row_copy(job, n).wait_send()
+            gather_copy(job, n).wait_send()
+        for n in range(len(ring.shifts)):
+            col_copy(job, n).wait_send()
 
 
 def transform_kernel(
     total, samples_ref, taps_ref, wh, wl, twc, tws, prod_ref, stats_ref,
-    raw, hraw, xf, tapb, y, v, u, pbuf, sums, part, rows_in, mine, cols_in, stat,
-    out_sems, in_sems, halo_send, halo_recv, row_send, row_recv, col_send, col_recv,
-    gat_send, gat_recv,
+    raw, hraw, xf, tapb, y, v, u, pbuf, sums,
+    part0, rows0, mine0, cols0, stat0, sems0, part1, rows1, mine1, cols1, stat1, sems1,
+    out_sems, in_sems, halo_send, halo_recv,
 ):
-    member, column, members, columns, cores = peers()
-    per = ROWS // members
-    count = members * columns
-    place = column * members + member
-    has_next = place < count - 1
+    MESH = pl.DeviceIdType.MESH
+    x_name, y_name, c_name = TM
+    nx, ny, nc = (lax.axis_size(n) for n in TM)
+    me = [lax.axis_index(n) for n in TM]
+    place = (me[0] * ny + me[1]) * nc + me[2]
+    has_next = place < nx * ny * nc - 1
     has_prev = place > 0
-    MESH = pl.DeviceIdType.MESH
 
     def tm_id(index):
-        return {"tm_0": index // members, **member_id(lax.rem(index, members), cores)}
+        return {
+            x_name: index // (ny * nc),
+            y_name: lax.rem(index // nc, ny),
+            c_name: lax.rem(index, nc),
+        }
+
+    barrier = pltpu.get_barrier_semaphore()
+    greeted = 0
+    for ring in rings():
+        for d, e in ring.steps:
+            if ring.half == 1 and d == 0:
+                continue
+            pl.semaphore_signal(
+                barrier, inc=1, device_id=ring.member_id(d, e), device_id_type=MESH
+            )
+            greeted += 1
+    row_start = jnp.logical_and(me[1] == 0, me[2] == 0)
+    row_end = jnp.logical_and(me[1] == ny - 1, me[2] == nc - 1)
+
+    @pl.when(jnp.logical_and(row_start, has_prev))
+    def _():
+        pl.semaphore_signal(barrier, inc=1, device_id=tm_id(place - 1), device_id_type=MESH)
 
     def in_copy(b):
         rows = pl.ds(pl.multiple_of(b * 256, 256), 256)
@@ -273,30 +414,13 @@
     for b in range(12):
         in_copy(b).start()
 
-    barrier = pltpu.get_barrier_semaphore()
-    for d in range(1, members):
-        other = lax.rem(member + d, members)
-        pl.semaphore_signal(
-            barrier, inc=1, device_id=member_id(other, cores), device_id_type=MESH
-        )
-    for d in range(1, columns):
-        other = lax.rem(column + d, columns)
-        pl.semaphore_signal(barrier, inc=1, device_id={"tm_0": other}, device_id_type=MESH)
-
-    first_member = member == 0
-    last_member = member == members - 1
-
-    @pl.when(jnp.logical_and(first_member, has_prev))
-    def _():
-        pl.semaphore_signal(barrier, inc=1, device_id=tm_id(place - 1), device_id_type=MESH)
-
-    greeted = members - 1 + columns - 1
-
-    @pl.when(jnp.logical_and(last_member, has_next))
+    more = jnp.logical_and(row_end, has_next)
+
+    @pl.when(more)
     def _():
         pl.semaphore_wait(barrier, greeted + 1)
 
-    @pl.when(jnp.logical_not(jnp.logical_and(last_member, has_next)))
+    @pl.when(jnp.logical_not(more))
     def _():
         pl.semaphore_wait(barrier, greeted)
 
@@ -307,13 +431,9 @@
         at = (4 * b + lead) * 64
         size = (4 - lead) * 64
         start = (frames - HALO) * 64 + at
-        return pltpu.make_async_remote_copy(
-            src_ref=samples_ref.at[:, pl.ds(start, size), :],
-            dst_ref=hraw.at[:, pl.ds(at, size), :],
-            send_sem=halo_send.at[b],
-            recv_sem=halo_recv.at[b],
-            device_id=tm_id(place + 1),
-            device_id_type=MESH,
+        return remote(
+            samples_ref.at[:, pl.ds(start, size), :], hraw.at[:, pl.ds(at, size), :],
+            halo_send.at[b], halo_recv.at[b], tm_id(place + 1),
         )
 
     @pl.when(has_next)
@@ -369,84 +489,19 @@
     transform(refs, 0, 1)
     out_copy(0).start()
 
-    for q in range(12):
-        for k1 in range(ROWS):
-            at = q * per + k1 % per
-            part[k1 // per, at : at + 1, :] = jnp.sum(
-                sums[q, k1 * 8 : k1 * 8 + 8, :], axis=0, keepdims=True
-            )
-
-    def row_copy(d):
-        other = lax.rem(member + d, members)
-        return pltpu.make_async_remote_copy(
-            src_ref=part.at[other],
-            dst_ref=rows_in.at[d - 1],
-            send_sem=row_send.at[d - 1],
-            recv_sem=row_recv.at[d - 1],
-            device_id=member_id(other, cores),
-            device_id_type=MESH,
-        )
-
-    for d in range(1, members):
-        row_copy(d).start()
-    acc = part[member]
-    for d in range(1, members):
-        row_copy(d).wait_recv()
-        acc = acc + rows_in[d - 1]
-    mine[...] = acc
-
-    def col_copy(d):
-        return pltpu.make_async_remote_copy(
-            src_ref=mine,
-            dst_ref=cols_in.at[d - 1],
-            send_sem=col_send.at[d - 1],
-            recv_sem=col_recv.at[d - 1],
-            device_id={"tm_0": lax.rem(column + d, columns)},
-            device_id_type=MESH,
-        )
-
-    for d in range(1, columns):
-        col_copy(d).start()
-    for d in range(1, columns):
-        col_copy(d).wait_recv()
-        acc = acc + cols_in[d - 1]
-    mean = acc * np.float32(1.0 / total)
-    power = [mean[per * s : per * (s + 1)] for s in range(4)]
-    coh = []
-    for p in range(4):
-        re = mean[per * (4 + p) : per * (5 + p)]
-        im = mean[per * (8 + p) : per * (9 + p)]
-        coh.append(
-            (re * re + im * im) / ((power[p // 2] + 1e-06) * (power[2 + p % 2] + 1e-06))
-        )
-    stat[...] = jnp.concatenate(power + coh, axis=0)
-    stats_ref[member] = stat[...]
-
-    def gather_copy(d):
-        return pltpu.make_async_remote_copy(
-            src_ref=stat,
-            dst_ref=stats_ref.at[member],
-            send_sem=gat_send.at[d - 1],
-            recv_sem=gat_recv.at[d - 1],
-            device_id=member_id(lax.rem(member + d, members), cores),
-            device_id_type=MESH,
-        )
-
-    for d in range(1, members):
-        gather_copy(d).start()
-    for d in range(1, members):
-        gather_copy(d).wait_recv()
+    all_reduce(
+        total, sums, stats_ref,
+        (
+            (part0, rows0, mine0, cols0, stat0, sems0),
+            (part1, rows1, mine1, cols1, stat1, sems1),
+        ),
+    )
 
     @pl.when(has_next)
     def _():
         for b in range(4):
             halo_copy(b).wait_send()
 
-    for d in range(1, members):
-        row_copy(d).wait_send()
-        gather_copy(d).wait_send()
-    for d in range(1, columns):
-        col_copy(d).wait_send()
     for n in range(3):
         out_copy(n).wait()
 
@@ -457,15 +512,22 @@
     vmem = pl.BlockSpec(memory_space=pltpu.VMEM)
     anywhere = pl.BlockSpec(memory_space=pl.ANY)
     f32, i32 = jnp.float32, jnp.int32
-    members = lax.axis_size(TM[1]) * lax.axis_size(TM[2])
-    columns = lax.axis_size(TM[0])
-    per = ROWS // members
     dma = pltpu.SemaphoreType.DMA
+    exchange = []
+    for ring in rings():
+        exchange += [
+            pltpu.VMEM((ring.members, ring.per, 3, 4, LANES), f32),
+            pltpu.VMEM((ring.members - 1, ring.per, 3, 4, LANES), f32),
+            pltpu.VMEM((ring.per, 3, 4, LANES), f32),
+            pltpu.VMEM((max(ring.nb - 1, 1), ring.per, 3, 4, LANES), f32),
+            pltpu.VMEM((ring.per, 2, 4, LANES), f32),
+            dma((6, max(ring.members, ring.nb) - 1)),
+        ]
     return pl.pallas_call(
         functools.partial(transform_kernel, total),
         out_shape=(
             jax.ShapeDtypeStruct((2, 4, frames, 4096), f32),
-            jax.ShapeDtypeStruct((members, 8 * per, LANES), f32),
+            jax.ShapeDtypeStruct((ROWS, 2, 4, LANES), f32),
         ),
         in_specs=[anywhere] + [vmem] * 5,
         out_specs=(anywhere, vmem),
@@ -479,21 +541,11 @@
             pltpu.VMEM((2, 16 * 37 * 8 + 16, LANES), f32),
             pltpu.VMEM((2, 4, frames, 4096 + LANES), f32),
             pltpu.VMEM((12, (ROWS + 1) * 8, LANES), f32),
-            pltpu.VMEM((members, 12 * per, LANES), f32),
-            pltpu.VMEM((members - 1, 12 * per, LANES), f32),
-            pltpu.VMEM((12 * per, LANES), f32),
-            pltpu.VMEM((columns - 1, 12 * per, LANES), f32),
-            pltpu.VMEM((8 * per, LANES), f32),
+            *exchange,
             dma((3,)),
             dma((12,)),
             dma((4,)),
             dma((4,)),
-            dma((members - 1,)),
-            dma((members - 1,)),
-            dma((columns - 1,)),
-            dma((columns - 1,)),
-            dma((members - 1,)),
-            dma((members - 1,)),
         ],
         compiler_params=pltpu.CompilerParams(
             vmem_limit_bytes=60 * 1024 * 1024, collective_id=0, has_side_effects=True
@@ -505,62 +557,67 @@
     )(rows, taps_rows, *consts)
 
 
-def normalize_kernel(stats_per, pairs_ref, stats_ref, prod_ref, coh_ref, out_ref):
-    pair = pl.program_id(0)
-    first = pairs_ref[0, pair]
-    second = pairs_ref[1, pair]
-    per = stats_per
-    members = ROWS // per
-
-    def stat(q, r):
-        return stats_ref[pl.ds(q * per + r, members, stride=8 * per), :]
-
-    for r in range(per):
-        power = (stat(first, r) + 1e-06) * (stat(second, r) + 1e-06)
-        factor = 1.0 / jnp.sqrt(power)
-        for m in range(members):
-            k1 = m * per + r
+def normalize_kernel(pairs_ref, stats_ref, prod_ref, coh_ref, out_ref, buf, factors, reads, writes):
+    def which(p):
+        return pairs_ref[0, p] * 2 + pairs_ref[1, p] - 2
+
+    def read(n):
+        p, part = n // 2, lax.rem(n, 2)
+        return pltpu.make_async_copy(prod_ref.at[part, which(p)], buf.at[n], reads.at[n])
+
+    def write(n):
+        p, part = n // 2, lax.rem(n, 2)
+        return pltpu.make_async_copy(buf.at[n], out_ref.at[part, p], writes.at[n])
+
+    for n in range(8):
+        read(n).start()
+
+    def stat(q):
+        return stats_ref[pl.ds(q, ROWS, stride=8), :]
+
+    for p in range(4):
+        power = (stat(pairs_ref[0, p]) + 1e-06) * (stat(pairs_ref[1, p]) + 1e-06)
+        factors[p * ROWS : (p + 1) * ROWS, :] = 1.0 / jnp.sqrt(power)
+        value = stat(4 + which(p))
+        for k1 in range(ROWS):
+            coh_ref[p : p + 1, k1 * LANES : (k1 + 1) * LANES] = value[k1 : k1 + 1]
+
+    def chunk(n, carry):
+        read(n).wait()
+        p = n // 2
+        factor = factors[pl.ds(pl.multiple_of(p * ROWS, ROWS), ROWS), :]
+        for k1 in range(ROWS):
             cols = slice(k1 * LANES, (k1 + 1) * LANES)
-            row = factor[m : m + 1]
-            for part in range(2):
-                out_ref[part, 0, :, cols] = prod_ref[part, 0, :, cols] * row
-
-    @pl.when(jnp.logical_and(pair == 0, pl.program_id(1) == 0))
-    def _():
-        for p in range(4):
-            which = pairs_ref[0, p] * 2 + pairs_ref[1, p] - 2
-            for r in range(per):
-                value = stat(4 + which, r)
-                for m in range(members):
-                    k1 = m * per + r
-                    coh_ref[p : p + 1, k1 * LANES : (k1 + 1) * LANES] = value[m : m + 1]
-
-
-def normalize_call(pairs, stats, prods, block=24):
+            buf[n, :, cols] = buf[n, :, cols] * factor[k1 : k1 + 1]
+        write(n).start()
+        return carry
+
+    lax.fori_loop(0, 8, chunk, 0)
+    for n in range(8):
+        write(n).wait()
+
+
+def normalize_call(pairs, stats, prods):
     frames = prods.shape[2]
     f32 = jnp.float32
     table = stats.reshape(-1, LANES)
+    vmem = pl.BlockSpec(memory_space=pltpu.VMEM)
+    anywhere = pl.BlockSpec(memory_space=pl.ANY)
     return pl.pallas_call(
-        functools.partial(normalize_kernel, stats.shape[1] // 8),
-        grid_spec=pltpu.PrefetchScalarGridSpec(
-            num_scalar_prefetch=1,
-            grid=(4, frames // block),
-            in_specs=[
-                pl.BlockSpec(table.shape, lambda p, b, pairs: (0, 0)),
-                pl.BlockSpec(
-                    (2, 1, block, 4096),
-                    lambda p, b, pairs: (0, pairs[0, p] * 2 + pairs[1, p] - 2, b, 0),
-                ),
-            ],
-            out_specs=[
-                pl.BlockSpec((4, 4096), lambda p, b, pairs: (0, 0)),
-                pl.BlockSpec((2, 1, block, 4096), lambda p, b, pairs: (0, p, b, 0)),
-            ],
-        ),
+        normalize_kernel,
+        in_specs=[pl.BlockSpec(memory_space=pltpu.SMEM), vmem, anywhere],
+        out_specs=(vmem, anywhere),
         out_shape=(
             jax.ShapeDtypeStruct((4, 4096), f32),
             jax.ShapeDtypeStruct(prods.shape, f32),
         ),
+        scratch_shapes=[
+            pltpu.VMEM((8, frames, 4096), f32),
+            pltpu.VMEM((4 * ROWS, LANES), f32),
+            pltpu.SemaphoreType.DMA((8,)),
+            pltpu.SemaphoreType.DMA((8,)),
+        ],
+        compiler_params=pltpu.CompilerParams(vmem_limit_bytes=60 * 1024 * 1024),
         cost_estimate=pl.CostEstimate(flops=2_000_000, bytes_accessed=13_000_000, transcendentals=0),
         name="normalize",
     )(pairs.T, table, prods)

time: 79.3 us -> 76 us (0.958)
  Pallas kernels: 78.4 us -> 75.2 us
    pallas_call x1, Pallas kernels: 8.81 us -> 7.1 us  [normalize_call(): pl.pallas_call(normalize_kernel, in_specs=[pl.BlockSpec(memory_space=pltp...]
    pallas_call x1, Pallas kernels: 69.5 us -> 68.1 us  [transform_call(): pl.pallas_call(functools.partial(transform_kernel, total), out_shape=(jax...]
where the time goes in v3:
time: 76 us; the launch traced here: 75.9 us
  Pallas kernels  75.2 us (99%)
    pallas_call x1, Pallas kernels, transform_call(): pl.pallas_call(functools.partial(transform_kernel, total), out_shape=(jax...  68.1 us
    pallas_call x1, Pallas kernels, normalize_call(): pl.pallas_call(normalize_kernel, in_specs=[pl.BlockSpec(memory_space=pltp...  7.1 us

profile of v3, /device:TPU:513, one launch (start us, length us, event | category | flops | bytes accessed | tf_op | source)
XLA Modules:
  0.0 75.9 jit_solution(3446329346174873941)
XLA Ops:
  0.6 68.1 %transform.1 = (f32[2,4,48,4096]{3,2,1,0:T(8,128)}, f32[32,2,4,128]{3,2,1,0:T(4,128)}) custom-call(s32[4,3072,128]{2,1,0:T(8,128)} %bitcast.14, f32[512,128]{1,0:T(8,128)} %bitcast.15, bf16[256,256]{1,0:T(8,128)(2,1)} %constant.8.clone.wh, bf16[256,256]{1,0:T(8,128)(2,1)} %constant.9.clone.wl, f32[32,128]{1,0:T(8,128)} %constant.10.clone.twc, ...), custom_call_target="tpu_custom_call" | custom-call | flops 4000000000 | bytes 16000000 | tf_op jit(solution)/shard_map/transform/pallas_call | solution.py:526
  68.8 7.1 %normalize.1 = (f32[4,4096]{1,0:T(4,128)}, f32[2,4,48,4096]{3,2,1,0:T(8,128)}) custom-call(s32[2,4]{1,0:T(2,128)} %bitcast.13, f32[256,128]{1,0:T(8,128)} %bitcast.12, f32[2,4,48,4096]{3,2,1,0:T(8,128)} %get-tuple-element.5.prod_ref), custom_call_target="tpu_custom_call" | custom-call | flops 2000000 | bytes 13000000 | tf_op jit(solution)/shard_map/normalize/pallas_call | solution.py:606

commit v4 on v3

--- a/solution.py
+++ b/solution.py
@@ -167,7 +167,7 @@
     lax.fori_loop(0, ROWS, body, 0)
 
 
-def transform(refs, group0, groups):
+def transform(refs, row_group, groups, fresh=False):
     (y, wh, wl, twc, tws, v, u, pbuf, sums) = refs
 
     def stage1(m, carry):
@@ -208,7 +208,11 @@
     def stage2b(n, carry):
         g = n // 8
         ka = lax.rem(n, 8)
-        rows = tile(group0 + g)
+        rows = tile(row_group + g)
+
+        def tally(q, value):
+            sums[q, at, :] = value if fresh else sums[q, at, :] + value
+
         spectra = []
         for s in range(4):
             xs = []
@@ -221,14 +225,14 @@
             z = [spectra[s][kb] for s in range(4)]
             at = tile(k1)
             for s in range(4):
-                sums[s, at, :] += z[s][0] * z[s][0] + z[s][1] * z[s][1]
+                tally(s, z[s][0] * z[s][0] + z[s][1] * z[s][1])
             cols = pl.ds(pl.multiple_of(k1 * LANES, LANES), LANES)
             for p in range(4):
                 a, b = z[p // 2], z[2 + p % 2]
                 re = a[0] * b[0] + a[1] * b[1]
                 im = a[1] * b[0] - a[0] * b[1]
-                sums[4 + p, at, :] += re
-                sums[8 + p, at, :] += im
+                tally(4 + p, re)
+                tally(8 + p, im)
                 pbuf[0, p, rows, cols] = re
                 pbuf[1, p, rows, cols] = im
         return carry
@@ -279,7 +283,7 @@
     )
 
 
-def all_reduce(total, sums, stats_ref, scratch):
+def all_reduce(total, sums, more, stats_ref, scratch, ready):
     both = rings()
     work = []
     for ring in both:
@@ -317,11 +321,18 @@
             for j in range(3):
                 part[k // ring.per, k % ring.per, j] = jnp.concatenate(
                     [
-                        jnp.sum(sums[4 * j + q, k1 * 8 : k1 * 8 + 8, :], axis=0, keepdims=True)
+                        jnp.sum(
+                            sums[4 * j + q, k1 * 8 : k1 * 8 + 8, :]
+                            + more[4 * j + q, k1 * 8 : k1 * 8 + 8, :],
+                            axis=0,
+                            keepdims=True,
+                        )
                         for q in range(4)
                     ],
                     axis=0,
                 )
+        if ring.half == 0:
+            ready()
         for n in range(len(ring.steps)):
             row_copy(job, n).start()
 
@@ -369,13 +380,10 @@
             col_copy(job, n).wait_send()
 
 
-def transform_kernel(
-    total, samples_ref, taps_ref, wh, wl, twc, tws, prod_ref, stats_ref,
-    raw, hraw, xf, tapb, y, v, u, pbuf, sums,
-    part0, rows0, mine0, cols0, stat0, sems0, part1, rows1, mine1, cols1, stat1, sems1,
-    out_sems, in_sems, halo_send, halo_recv,
+def filter_kernel(
+    samples_ref, taps_ref, wh, wl, twc, tws, prod_ref, y0_ref, sums,
+    raw, hraw, xf, tapb, y, v, u, in_sems, halo_send, halo_recv,
 ):
-    MESH = pl.DeviceIdType.MESH
     x_name, y_name, c_name = TM
     nx, ny, nc = (lax.axis_size(n) for n in TM)
     me = [lax.axis_index(n) for n in TM]
@@ -391,38 +399,12 @@
         }
 
     barrier = pltpu.get_barrier_semaphore()
-    greeted = 0
-    for ring in rings():
-        for d, e in ring.steps:
-            if ring.half == 1 and d == 0:
-                continue
-            pl.semaphore_signal(
-                barrier, inc=1, device_id=ring.member_id(d, e), device_id_type=MESH
-            )
-            greeted += 1
-    row_start = jnp.logical_and(me[1] == 0, me[2] == 0)
-    row_end = jnp.logical_and(me[1] == ny - 1, me[2] == nc - 1)
-
-    @pl.when(jnp.logical_and(row_start, has_prev))
+
+    @pl.when(has_prev)
     def _():
-        pl.semaphore_signal(barrier, inc=1, device_id=tm_id(place - 1), device_id_type=MESH)
-
-    def in_copy(b):
-        rows = pl.ds(pl.multiple_of(b * 256, 256), 256)
-        return pltpu.make_async_copy(samples_ref.at[:, rows, :], raw.at[:, rows, :], in_sems.at[b])
-
-    for b in range(12):
-        in_copy(b).start()
-
-    more = jnp.logical_and(row_end, has_next)
-
-    @pl.when(more)
-    def _():
-        pl.semaphore_wait(barrier, greeted + 1)
-
-    @pl.when(jnp.logical_not(more))
-    def _():
-        pl.semaphore_wait(barrier, greeted)
+        pl.semaphore_signal(
+            barrier, inc=1, device_id=tm_id(place - 1), device_id_type=pl.DeviceIdType.MESH
+        )
 
     frames = samples_ref.shape[1] // 64
 
@@ -436,8 +418,18 @@
             halo_send.at[b], halo_recv.at[b], tm_id(place + 1),
         )
 
+    def in_copy(b):
+        rows = pl.ds(pl.multiple_of(b * 256, 256), 256)
+        return pltpu.make_async_copy(samples_ref.at[:, rows, :], raw.at[:, rows, :], in_sems.at[b])
+
+    for b in range(12):
+        in_copy(b).start()
+
+    permute_taps(taps_ref, tapb)
+
     @pl.when(has_next)
     def _():
+        pl.semaphore_wait(barrier, 1)
         for b in (3, 2, 1, 0):
             halo_copy(b).start()
 
@@ -451,9 +443,8 @@
             halo_copy(b).wait_recv()
 
     filters = (xf, tapb, y)
-    refs = (y, wh, wl, twc, tws, v, u, pbuf, sums)
+    refs = (y, wh, wl, twc, tws, v, u, prod_ref, sums)
     sums[...] = jnp.zeros_like(sums)
-    permute_taps(taps_ref, tapb)
 
     def own_batch(b, carry):
         in_copy(b).wait()
@@ -462,56 +453,103 @@
 
     lax.fori_loop(0, 12, own_batch, 0)
 
-    def out_copy(n):
-        rows = (pl.ds(0, 8), pl.ds(8, 8), pl.ds(16, frames - 16))[n]
-        return pltpu.make_async_copy(
-            pbuf.at[:, :, rows, pl.ds(0, 4096)], prod_ref.at[:, :, rows, :], out_sems.at[n]
-        )
-
     fir(filters, 2, 4, 0, 16)
-    transform(refs, 2, 4)
-    out_copy(2).start()
+    transform(refs, 1, 4)
 
     halo_wait(3)
     halo_wait(2)
     permute_batch(hraw, xf, 3, 0)
     permute_batch(hraw, xf, 2, 0)
     fir(filters, 1, 1, 0, 16)
-    transform(refs, 1, 1)
-    out_copy(1).start()
-
+    transform(refs, 0, 1)
+
+    filters = (xf, tapb, y0_ref)
     halo_wait(1)
     permute_batch(hraw, xf, 1, 0)
     fir(filters, 0, 1, 0, 13)
     halo_wait(0)
     permute_batch(hraw, xf, 0, 0)
     fir(filters, 0, 1, 13, 16, extend=True)
-    transform(refs, 0, 1)
-    out_copy(0).start()
-
-    all_reduce(
-        total, sums, stats_ref,
-        (
-            (part0, rows0, mine0, cols0, stat0, sems0),
-            (part1, rows1, mine1, cols1, stat1, sems1),
-        ),
-    )
 
     @pl.when(has_next)
     def _():
         for b in range(4):
             halo_copy(b).wait_send()
 
-    for n in range(3):
-        out_copy(n).wait()
-
-
-def transform_call(rows, taps_rows, total):
+
+def reduce_kernel(
+    total, y0, sums_ref, wh, wl, twc, tws, prod_ref, stats_ref,
+    v, u, sums, part0, rows0, mine0, cols0, stat0, sems0,
+    part1, rows1, mine1, cols1, stat1, sems1,
+):
+    barrier = pltpu.get_barrier_semaphore()
+    greeted = 0
+    for ring in rings():
+        for d, e in ring.steps:
+            if ring.half == 1 and d == 0:
+                continue
+            pl.semaphore_signal(
+                barrier,
+                inc=1,
+                device_id=ring.member_id(d, e),
+                device_id_type=pl.DeviceIdType.MESH,
+            )
+            greeted += 1
+
+    transform((y0, wh, wl, twc, tws, v, u, prod_ref, sums), 0, 1, fresh=True)
+    all_reduce(
+        total, sums, sums_ref, stats_ref,
+        (
+            (part0, rows0, mine0, cols0, stat0, sems0),
+            (part1, rows1, mine1, cols1, stat1, sems1),
+        ),
+        lambda: pl.semaphore_wait(barrier, greeted),
+    )
+
+
+VMEM_ALL = pl.BlockSpec(memory_space=pltpu.VMEM)
+ANYWHERE = pl.BlockSpec(memory_space=pl.ANY)
+WIDE = 4096 + LANES
+MIB = 1024 * 1024
+
+
+def filter_call(rows, taps_rows, consts):
     frames = rows.shape[1] // 64
-    consts = [jnp.asarray(c) for c in constants()]
-    vmem = pl.BlockSpec(memory_space=pltpu.VMEM)
-    anywhere = pl.BlockSpec(memory_space=pl.ANY)
     f32, i32 = jnp.float32, jnp.int32
+    dma = pltpu.SemaphoreType.DMA
+    return pl.pallas_call(
+        filter_kernel,
+        out_shape=(
+            jax.ShapeDtypeStruct((2, 4, frames - GROUP, WIDE), f32),
+            jax.ShapeDtypeStruct((1024, 256), f32),
+            jax.ShapeDtypeStruct((12, (ROWS + 1) * 8, LANES), f32),
+        ),
+        in_specs=[ANYWHERE] + [VMEM_ALL] * 5,
+        out_specs=(VMEM_ALL, VMEM_ALL, VMEM_ALL),
+        scratch_shapes=[
+            pltpu.VMEM((4, frames * 64, LANES), i32),
+            pltpu.VMEM((4, HALO * 64, LANES), i32),
+            pltpu.VMEM((8, ROWS * PITCH + 7, LANES), f32),
+            pltpu.VMEM((ROWS * 16 * 8, LANES), f32),
+            pltpu.VMEM((4096, 256), f32),
+            pltpu.VMEM((4096, 256), f32),
+            pltpu.VMEM((2, 16 * 37 * 8 + 16, LANES), f32),
+            dma((12,)),
+            dma((4,)),
+            dma((4,)),
+        ],
+        compiler_params=pltpu.CompilerParams(
+            vmem_limit_bytes=45 * MIB, collective_id=0, has_side_effects=True
+        ),
+        cost_estimate=pl.CostEstimate(
+            flops=4_000_000_000, bytes_accessed=16_000_000, transcendentals=0
+        ),
+        name="filter",
+    )(rows, taps_rows, *consts)
+
+
+def reduce_call(y0, sums, consts, total):
+    f32 = jnp.float32
     dma = pltpu.SemaphoreType.DMA
     exchange = []
     for ring in rings():
@@ -524,103 +562,82 @@
             dma((6, max(ring.members, ring.nb) - 1)),
         ]
     return pl.pallas_call(
-        functools.partial(transform_kernel, total),
+        functools.partial(reduce_kernel, total),
         out_shape=(
-            jax.ShapeDtypeStruct((2, 4, frames, 4096), f32),
+            jax.ShapeDtypeStruct((2, 4, GROUP, WIDE), f32),
             jax.ShapeDtypeStruct((ROWS, 2, 4, LANES), f32),
         ),
-        in_specs=[anywhere] + [vmem] * 5,
-        out_specs=(anywhere, vmem),
+        in_specs=[VMEM_ALL] * 6,
+        out_specs=(VMEM_ALL, VMEM_ALL),
         scratch_shapes=[
-            pltpu.VMEM((4, frames * 64, LANES), i32),
-            pltpu.VMEM((4, HALO * 64, LANES), i32),
-            pltpu.VMEM((8, ROWS * PITCH + 7, LANES), f32),
-            pltpu.VMEM((ROWS * 16 * 8, LANES), f32),
-            pltpu.VMEM((4096, 256), f32),
-            pltpu.VMEM((4096, 256), f32),
-            pltpu.VMEM((2, 16 * 37 * 8 + 16, LANES), f32),
-            pltpu.VMEM((2, 4, frames, 4096 + LANES), f32),
+            pltpu.VMEM((1024, 256), f32),
+            pltpu.VMEM((2, 4 * 37 * 8 + 16, LANES), f32),
             pltpu.VMEM((12, (ROWS + 1) * 8, LANES), f32),
             *exchange,
-            dma((3,)),
-            dma((12,)),
-            dma((4,)),
-            dma((4,)),
         ],
         compiler_params=pltpu.CompilerParams(
-            vmem_limit_bytes=60 * 1024 * 1024, collective_id=0, has_side_effects=True
+            vmem_limit_bytes=16 * MIB, collective_id=1, has_side_effects=True
         ),
         cost_estimate=pl.CostEstimate(
-            flops=4_000_000_000, bytes_accessed=16_000_000, transcendentals=0
-        ),
-        name="transform",
-    )(rows, taps_rows, *consts)
-
-
-def normalize_kernel(pairs_ref, stats_ref, prod_ref, coh_ref, out_ref, buf, factors, reads, writes):
-    def which(p):
-        return pairs_ref[0, p] * 2 + pairs_ref[1, p] - 2
-
-    def read(n):
-        p, part = n // 2, lax.rem(n, 2)
-        return pltpu.make_async_copy(prod_ref.at[part, which(p)], buf.at[n], reads.at[n])
-
-    def write(n):
-        p, part = n // 2, lax.rem(n, 2)
-        return pltpu.make_async_copy(buf.at[n], out_ref.at[part, p], writes.at[n])
-
-    for n in range(8):
-        read(n).start()
+            flops=400_000_000, bytes_accessed=3_000_000, transcendentals=0
+        ),
+        name="reduce",
+    )(y0, sums, *consts)
+
+
+def normalize_kernel(pairs_ref, stats_ref, first_ref, rest_ref, coh_ref, out_ref, buf, writes):
+    frames = buf.shape[2]
+
+    def write(p, part):
+        return pltpu.make_async_copy(
+            buf.at[p, part], out_ref.at[part, p], writes.at[2 * p + part]
+        )
 
     def stat(q):
         return stats_ref[pl.ds(q, ROWS, stride=8), :]
 
+    def pair(p, carry):
+        which = pairs_ref[0, p] * 2 + pairs_ref[1, p] - 2
+        power = (stat(pairs_ref[0, p]) + 1e-06) * (stat(pairs_ref[1, p]) + 1e-06)
+        factor = 1.0 / jnp.sqrt(power)
+        for part in range(2):
+            for k1 in range(ROWS):
+                cols = slice(k1 * LANES, (k1 + 1) * LANES)
+                row = factor[k1 : k1 + 1]
+                buf[p, part, 0:GROUP, cols] = first_ref[part, which, :, cols] * row
+                buf[p, part, GROUP:frames, cols] = rest_ref[part, which, :, cols] * row
+            write(p, part).start()
+        return carry
+
+    lax.fori_loop(0, 4, pair, 0)
     for p in range(4):
-        power = (stat(pairs_ref[0, p]) + 1e-06) * (stat(pairs_ref[1, p]) + 1e-06)
-        factors[p * ROWS : (p + 1) * ROWS, :] = 1.0 / jnp.sqrt(power)
-        value = stat(4 + which(p))
+        value = stat(4 + pairs_ref[0, p] * 2 + pairs_ref[1, p] - 2)
         for k1 in range(ROWS):
             coh_ref[p : p + 1, k1 * LANES : (k1 + 1) * LANES] = value[k1 : k1 + 1]
-
-    def chunk(n, carry):
-        read(n).wait()
-        p = n // 2
-        factor = factors[pl.ds(pl.multiple_of(p * ROWS, ROWS), ROWS), :]
-        for k1 in range(ROWS):
-            cols = slice(k1 * LANES, (k1 + 1) * LANES)
-            buf[n, :, cols] = buf[n, :, cols] * factor[k1 : k1 + 1]
-        write(n).start()
-        return carry
-
-    lax.fori_loop(0, 8, chunk, 0)
-    for n in range(8):
-        write(n).wait()
-
-
-def normalize_call(pairs, stats, prods):
-    frames = prods.shape[2]
+    for p in range(4):
+        for part in range(2):
+            write(p, part).wait()
+
+
+def normalize_call(pairs, stats, first, rest):
+    frames = first.shape[2] + rest.shape[2]
     f32 = jnp.float32
-    table = stats.reshape(-1, LANES)
-    vmem = pl.BlockSpec(memory_space=pltpu.VMEM)
-    anywhere = pl.BlockSpec(memory_space=pl.ANY)
     return pl.pallas_call(
         normalize_kernel,
-        in_specs=[pl.BlockSpec(memory_space=pltpu.SMEM), vmem, anywhere],
-        out_specs=(vmem, anywhere),
+        in_specs=[pl.BlockSpec(memory_space=pltpu.SMEM)] + [VMEM_ALL] * 3,
+        out_specs=(VMEM_ALL, ANYWHERE),
         out_shape=(
             jax.ShapeDtypeStruct((4, 4096), f32),
-            jax.ShapeDtypeStruct(prods.shape, f32),
+            jax.ShapeDtypeStruct((2, 4, frames, 4096), f32),
         ),
         scratch_shapes=[
-            pltpu.VMEM((8, frames, 4096), f32),
-            pltpu.VMEM((4 * ROWS, LANES), f32),
-            pltpu.SemaphoreType.DMA((8,)),
+            pltpu.VMEM((4, 2, frames, 4096), f32),
             pltpu.SemaphoreType.DMA((8,)),
         ],
-        compiler_params=pltpu.CompilerParams(vmem_limit_bytes=60 * 1024 * 1024),
+        compiler_params=pltpu.CompilerParams(vmem_limit_bytes=20 * MIB),
         cost_estimate=pl.CostEstimate(flops=2_000_000, bytes_accessed=13_000_000, transcendentals=0),
         name="normalize",
-    )(pairs.T, table, prods)
+    )(pairs.T, stats.reshape(-1, LANES), first, rest)
 
 
 def sample_rows(volts):
@@ -637,8 +654,10 @@
 def on_device(volts, taps, pairs):
     rows = sample_rows(volts)
     total = rows.shape[1] // 64 * lax.axis_size(TM)
-    prods, stats = transform_call(rows, tap_rows(taps), total)
-    return normalize_call(pairs, stats, prods)
+    consts = [jnp.asarray(c) for c in constants()]
+    rest, y0, sums = filter_call(rows, tap_rows(taps), consts)
+    first, stats = reduce_call(y0, sums, consts, total)
+    return normalize_call(pairs, stats, first, rest)
 
 
 def solution(mesh):

time: 76 us -> 70.5 us (0.928)
  Pallas kernels: 75.2 us -> 65.3 us
  local copies, waits for them, and re-layouts: 0 us -> 4.19 us
    pallas_call x1 -> x2, Pallas kernels: 68.1 us -> 61.3 us  [the longest x1 30.8 us: reduce_call(): pl.pallas_call(functools.partial(reduce_kernel, total), out_shape=(jax.Sh...]
    unnamed x0 -> x12, local copies, waits for them, and re-layouts: none -> 4.19 us
    pallas_call x1, Pallas kernels: 7.1 us -> 4.01 us  [normalize_call(): pl.pallas_call(normalize_kernel, in_specs=[pl.BlockSpec(memory_space=pltp...]
where the time goes in v4:
time: 70.5 us; the launch traced here: 70.2 us
  Pallas kernels  65.3 us (93%)
  local copies, waits for them, and re-layouts  4.19 us (6%)
    pallas_call x1, Pallas kernels, reduce_call(): pl.pallas_call(functools.partial(reduce_kernel, total), out_shape=(jax.Sh...  30.8 us
    pallas_call x1, Pallas kernels, filter_call(): pl.pallas_call(filter_kernel, out_shape=(jax.ShapeDtypeStruct((2, 4, fram...  30.6 us
    unnamed x12, local copies, waits for them, and re-layouts  4.19 us
    pallas_call x1, Pallas kernels, normalize_call(): pl.pallas_call(normalize_kernel, in_specs=[pl.BlockSpec(memory_space=pltp...  4.01 us

profile of v4, /device:TPU:513, one launch (start us, length us, event | category | flops | bytes accessed | tf_op | source)
XLA Modules:
  0.0 70.2 jit_solution(14063835622511128705)
XLA Ops:
  0.6 0.0 copy-start
  0.6 0.9 %copy-done = bf16[256,256]{1,0:T(8,128)(2,1)S(1)} copy-done((bf16[256,256]{1,0:T(8,128)(2,1)S(1)}, bf16[256,256]{1,0:T(8,128)(2,1)}, u32[]{:S(2)}) %copy-start) | copy-done | bytes 131096
  1.5 0.0 copy-start.1
  1.5 0.9 %copy-done.1 = bf16[256,256]{1,0:T(8,128)(2,1)S(1)} copy-done((bf16[256,256]{1,0:T(8,128)(2,1)S(1)}, bf16[256,256]{1,0:T(8,128)(2,1)}, u32[]{:S(2)}) %copy-start.1) | copy-done | bytes 131096
  2.4 0.0 copy-start.2
  2.4 0.7 %copy-done.2 = f32[32,128]{1,0:T(8,128)S(1)} copy-done((f32[32,128]{1,0:T(8,128)S(1)}, f32[32,128]{1,0:T(8,128)}, u32[]{:S(2)}) %copy-start.2) | copy-done | bytes 16408
  3.2 0.0 copy-start.3
  3.2 0.7 %copy-done.3 = f32[32,128]{1,0:T(8,128)S(1)} copy-done((f32[32,128]{1,0:T(8,128)S(1)}, f32[32,128]{1,0:T(8,128)}, u32[]{:S(2)}) %copy-start.3) | copy-done | bytes 16408
  3.9 0.0 copy-start.5
  3.9 0.9 %copy-done.5 = f32[16,4096]{1,0:T(8,128)S(1)} copy-done((f32[16,4096]{1,0:T(8,128)S(1)}, f32[16,4096]{1,0:T(8,128)}, u32[]{:S(2)}) %copy-start.5) | copy-done | bytes 262168
  4.8 0.0 copy-start.4
  4.8 30.6 %filter.1 = (f32[2,4,40,4224]{3,2,1,0:T(8,128)S(1)}, f32[1024,256]{1,0:T(8,128)S(1)}, f32[12,264,128]{2,1,0:T(8,128)S(1)}) custom-call(s32[4,3072,128]{2,1,0:T(8,128)} %bitcast.15, f32[512,128]{1,0:T(8,128)S(1)} %bitcast.14, bf16[256,256]{1,0:T(8,128)(2,1)S(1)} %copy-done.1, bf16[256,256]{1,0:T(8,128)(2,1)S(1)} %copy-done, f32[32,128]{1,0:T(8,128)S(1)} %copy-done.3, ...), custom_call_target="tpu_custom_call" | custom-call | flops 4000000000 | bytes 16000000 | tf_op jit(solution)/shard_map/filter/pallas_call | solution.py:520
  35.4 30.8 %reduce.1 = (f32[2,4,8,4224]{3,2,1,0:T(8,128)S(1)}, f32[32,2,4,128]{3,2,1,0:T(4,128)S(1)}) custom-call(f32[1024,256]{1,0:T(8,128)S(1)} %get-tuple-element.7.y0, f32[12,264,128]{2,1,0:T(8,128)S(1)} %get-tuple-element.8.sums_ref, bf16[256,256]{1,0:T(8,128)(2,1)S(1)} %copy-done.1, bf16[256,256]{1,0:T(8,128)(2,1)S(1)} %copy-done, f32[32,128]{1,0:T(8,128)S(1)} %copy-done.3, ...), custom_call_target="tpu_custom_call" | custom-call | flops 400000000 | bytes 3000000 | tf_op jit(solution)/shard_map/reduce/pallas_call | solution.py:564
  66.2 0.0 copy-done.4
  66.2 4.0 %normalize.1 = (f32[4,4096]{1,0:T(4,128)}, f32[2,4,48,4096]{3,2,1,0:T(8,128)}) custom-call(s32[2,4]{1,0:T(2,128)S(1)} %bitcast.13, f32[256,128]{1,0:T(8,128)S(1)} %bitcast.12, f32[2,4,8,4224]{3,2,1,0:T(8,128)S(1)} %get-tuple-element.10.first_ref, f32[2,4,40,4224]{3,2,1,0:T(8,128)S(1)} %get-tuple-element.11.rest_ref), custom_call_target="tpu_custom_call" | custom-call | flops 2000000 | bytes 13000000 | tf_op jit(solution)/shard_map/normalize/pallas_call | solution.py:625
Async XLA Ops:
  0.6 0.9 %copy-start = (bf16[256,256]{1,0:T(8,128)(2,1)S(1)}, bf16[256,256]{1,0:T(8,128)(2,1)}, u32[]{:S(2)}) copy-start(bf16[256,256]{1,0:T(8,128)(2,1)} %constant.9.clone.wl) | copy-start | bytes 393220
  1.5 0.9 %copy-start.1 = (bf16[256,256]{1,0:T(8,128)(2,1)S(1)}, bf16[256,256]{1,0:T(8,128)(2,1)}, u32[]{:S(2)}) copy-start(bf16[256,256]{1,0:T(8,128)(2,1)} %constant.8.clone.wh) | copy-start | bytes 393220
  2.4 0.7 %copy-start.2 = (f32[32,128]{1,0:T(8,128)S(1)}, f32[32,128]{1,0:T(8,128)}, u32[]{:S(2)}) copy-start(f32[32,128]{1,0:T(8,128)} %constant.11.clone.tws) | copy-start | bytes 49156
  3.2 0.7 %copy-start.3 = (f32[32,128]{1,0:T(8,128)S(1)}, f32[32,128]{1,0:T(8,128)}, u32[]{:S(2)}) copy-start(f32[32,128]{1,0:T(8,128)} %constant.10.clone.twc) | copy-start | bytes 49156
  3.9 0.9 %copy-start.5 = (f32[16,4096]{1,0:T(8,128)S(1)}, f32[16,4096]{1,0:T(8,128)}, u32[]{:S(2)}) copy-start(f32[16,4096]{1,0:T(8,128)} %param.8) | copy-start | bytes 786436
  4.8 61.4 %copy-start.4 = (s32[4,2]{0,1:T(2,128)S(1)}, s32[4,2]{0,1:T(2,128)}, u32[]{:S(2)}) copy-start(s32[4,2]{0,1:T(2,128)} %param.9) | copy-start | bytes 100

commit v5 on v4

--- a/solution.py
+++ b/solution.py
@@ -18,23 +18,24 @@
 GROUP = 8
 
 
-def constants():
-    lane = np.arange(LANES)
-    j = 4 * (lane % 32) + lane // 32
-    k = np.arange(LANES)
-    angle = 2.0 * np.pi * ((j[:, None] * k[None, :]) % LANES) / LANES
-    cos, sin = np.cos(angle) / 64.0, np.sin(angle) / 64.0
-    full = np.block([[cos, -sin], [sin, cos]]).astype(np.float32)
-    high = full.astype(jnp.bfloat16)
-    low = (full - high.astype(np.float32)).astype(jnp.bfloat16)
-    i = np.arange(ROWS)
-    turn = 2.0 * np.pi * ((i[:, None] * k[None, :]) % 4096) / 4096
-    return (
-        high,
-        low,
-        np.cos(turn).astype(np.float32),
-        np.sin(turn).astype(np.float32),
-    )
+def fill_tables(wh, wl, twc, tws):
+    row = lax.broadcasted_iota(jnp.int32, (LANES, LANES), 0)
+    k = lax.broadcasted_iota(jnp.int32, (LANES, LANES), 1)
+    j = 4 * (row & 31) + (row >> 5)
+    angle = ((j * k) & (LANES - 1)).astype(jnp.float32) * np.float32(2.0 * math.pi / LANES)
+    cos, sin = jnp.cos(angle) * np.float32(1 / 64), jnp.sin(angle) * np.float32(1 / 64)
+    low, high = slice(0, LANES), slice(LANES, 2 * LANES)
+    for rows, cols, value in (
+        (low, low, cos), (low, high, -sin), (high, low, sin), (high, high, cos),
+    ):
+        head = value.astype(jnp.bfloat16)
+        wh[rows, cols] = head
+        wl[rows, cols] = (value - head.astype(jnp.float32)).astype(jnp.bfloat16)
+    i = lax.broadcasted_iota(jnp.int32, (ROWS, LANES), 0)
+    k = lax.broadcasted_iota(jnp.int32, (ROWS, LANES), 1)
+    turn = (i * k).astype(jnp.float32) * np.float32(2.0 * math.pi / 4096)
+    twc[...] = jnp.cos(turn)
+    tws[...] = jnp.sin(turn)
 
 
 def add(a, b):
@@ -144,24 +145,27 @@
         tap = {
             t: tapb[pl.ds(pl.multiple_of((i * 16 + t) * 8, 8), 8), :] for t in range(tap0, tap1)
         }
-        for c in range(2):
-            cols = slice(c * LANES, (c + 1) * LANES)
-            for s in range(4):
-                at = [
-                    pl.ds(pl.multiple_of((g * 128 + s * 32 + place) * 8, 8), 8)
-                    for g in range(groups)
-                ]
-                acc = [y[at[g], cols] if extend else None for g in range(groups)]
-                for w in range(1 - tap1, 8 * (groups - 1) - tap0 + 1):
-                    users = [g for g in range(groups) if tap0 <= 8 * g - w < tap1]
-                    if not users:
-                        continue
-                    x = xf[2 * s + c, pl.ds(base + w, 8), :]
-                    for g in users:
-                        term = tap[8 * g - w] * x
-                        acc[g] = term if acc[g] is None else acc[g] + term
-                for g in range(groups):
-                    y[at[g], cols] = acc[g]
+        for s in range(4):
+            at = [
+                pl.ds(pl.multiple_of((g * 128 + s * 32 + place) * 8, 8), 8)
+                for g in range(groups)
+            ]
+            cols = [slice(c * LANES, (c + 1) * LANES) for c in range(2)]
+            acc = [
+                [y[at[g], cols[c]] if extend else None for c in range(2)] for g in range(groups)
+            ]
+            for w in range(1 - tap1, 8 * (groups - 1) - tap0 + 1):
+                users = [g for g in range(groups) if tap0 <= 8 * g - w < tap1]
+                if not users:
+                    continue
+                x = [xf[2 * s + c, pl.ds(base + w, 8), :] for c in range(2)]
+                for g in users:
+                    for c in range(2):
+                        term = tap[8 * g - w] * x[c]
+                        acc[g][c] = term if acc[g][c] is None else acc[g][c] + term
+            for g in range(groups):
+                for c in range(2):
+                    y[at[g], cols[c]] = acc[g][c]
         return carry
 
     lax.fori_loop(0, ROWS, body, 0)
@@ -171,7 +175,7 @@
     (y, wh, wl, twc, tws, v, u, pbuf, sums) = refs
 
     def stage1(m, carry):
-        at = pl.ds(pl.multiple_of(m * 512, 512), 512)
+        at = pl.ds(pl.multiple_of(m * 1024, 1024), 1024)
         x = y[at, :]
         h = x.astype(jnp.bfloat16)
         l = (x - h.astype(jnp.float32)).astype(jnp.bfloat16)
@@ -179,7 +183,7 @@
         v[at, :] = dot(h, wh[...]) + dot(l, wh[...]) + dot(h, wl[...])
         return carry
 
-    lax.fori_loop(0, 2 * groups, stage1, 0)
+    lax.fori_loop(0, groups, stage1, 0)
 
     def tile(n):
         return pl.ds(pl.multiple_of(n * 8, 8), 8)
@@ -381,7 +385,8 @@
 
 
 def filter_kernel(
-    samples_ref, taps_ref, wh, wl, twc, tws, prod_ref, y0_ref, sums,
+    samples_ref, taps_ref,
+    prod_ref, y0_ref, sums, wh, wl, twc, tws,
     raw, hraw, xf, tapb, y, v, u, in_sems, halo_send, halo_recv,
 ):
     x_name, y_name, c_name = TM
@@ -425,8 +430,6 @@
     for b in range(12):
         in_copy(b).start()
 
-    permute_taps(taps_ref, tapb)
-
     @pl.when(has_next)
     def _():
         pl.semaphore_wait(barrier, 1)
@@ -445,6 +448,8 @@
     filters = (xf, tapb, y)
     refs = (y, wh, wl, twc, tws, v, u, prod_ref, sums)
     sums[...] = jnp.zeros_like(sums)
+    fill_tables(wh, wl, twc, tws)
+    permute_taps(taps_ref, tapb)
 
     def own_batch(b, carry):
         in_copy(b).wait()
@@ -513,7 +518,7 @@
 MIB = 1024 * 1024
 
 
-def filter_call(rows, taps_rows, consts):
+def filter_call(rows, taps_rows):
     frames = rows.shape[1] // 64
     f32, i32 = jnp.float32, jnp.int32
     dma = pltpu.SemaphoreType.DMA
@@ -523,9 +528,11 @@
             jax.ShapeDtypeStruct((2, 4, frames - GROUP, WIDE), f32),
             jax.ShapeDtypeStruct((1024, 256), f32),
             jax.ShapeDtypeStruct((12, (ROWS + 1) * 8, LANES), f32),
-        ),
-        in_specs=[ANYWHERE] + [VMEM_ALL] * 5,
-        out_specs=(VMEM_ALL, VMEM_ALL, VMEM_ALL),
+            *[jax.ShapeDtypeStruct((256, 256), jnp.bfloat16)] * 2,
+            *[jax.ShapeDtypeStruct((ROWS, LANES), f32)] * 2,
+        ),
+        in_specs=[ANYWHERE, VMEM_ALL],
+        out_specs=(VMEM_ALL,) * 7,
         scratch_shapes=[
             pltpu.VMEM((4, frames * 64, LANES), i32),
             pltpu.VMEM((4, HALO * 64, LANES), i32),
@@ -545,7 +552,7 @@
             flops=4_000_000_000, bytes_accessed=16_000_000, transcendentals=0
         ),
         name="filter",
-    )(rows, taps_rows, *consts)
+    )(rows, taps_rows)
 
 
 def reduce_call(y0, sums, consts, total):
@@ -654,9 +661,8 @@
 def on_device(volts, taps, pairs):
     rows = sample_rows(volts)
     total = rows.shape[1] // 64 * lax.axis_size(TM)
-    consts = [jnp.asarray(c) for c in constants()]
-    rest, y0, sums = filter_call(rows, tap_rows(taps), consts)
-    first, stats = reduce_call(y0, sums, consts, total)
+    rest, y0, sums, *held = filter_call(rows, tap_rows(taps))
+    first, stats = reduce_call(y0, sums, held, total)
     return normalize_call(pairs, stats, first, rest)
 
 

time: 70.5 us -> 66 us (0.936)
  local copies, waits for them, and re-layouts: 4.19 us -> 0.95 us
  Pallas kernels: 65.3 us -> 64.3 us
    unnamed x12 -> x4, local copies, waits for them, and re-layouts: 4.19 us -> 0.95 us
    pallas_call x1, Pallas kernels: 30.6 us -> 29 us  [filter_call(): pl.pallas_call(filter_kernel, out_shape=(jax.ShapeDtypeStruct((2, 4, fram...]
where the time goes in v5:
time: 66 us; the launch traced here: 65.9 us
  Pallas kernels  64.3 us (97%)
  local copies, waits for them, and re-layouts  0.95 us (1%)
  between operations  0.66 us (1%)
    pallas_call x1, Pallas kernels, reduce_call(): pl.pallas_call(functools.partial(reduce_kernel, total), out_shape=(jax.Sh...  31.3 us
    pallas_call x1, Pallas kernels, filter_call(): pl.pallas_call(filter_kernel, out_shape=(jax.ShapeDtypeStruct((2, 4, fram...  29 us
    pallas_call x1, Pallas kernels, normalize_call(): pl.pallas_call(normalize_kernel, in_specs=[pl.BlockSpec(memory_space=pltp...  4.01 us

profile of v5, /device:TPU:513, one launch (start us, length us, event | category | flops | bytes accessed | tf_op | source)
XLA Modules:
  0.0 65.9 jit_solution(2868467706252539823)
XLA Ops:
  0.6 0.0 copy-start.1
  0.6 0.9 %copy-done.1 = f32[16,4096]{1,0:T(8,128)S(1)} copy-done((f32[16,4096]{1,0:T(8,128)S(1)}, f32[16,4096]{1,0:T(8,128)}, u32[]{:S(2)}) %copy-start.1) | copy-done | bytes 262168
  1.6 0.0 copy-start
  1.6 29.0 %filter.1 = (f32[2,4,40,4224]{3,2,1,0:T(8,128)S(1)}, f32[1024,256]{1,0:T(8,128)S(1)}, f32[12,264,128]{2,1,0:T(8,128)S(1)}, bf16[256,256]{1,0:T(8,128)(2,1)S(1)},...) custom-call(s32[4,3072,128]{2,1,0:T(8,128)} %bitcast.15, f32[512,128]{1,0:T(8,128)S(1)} %bitcast.14), custom_call_target="tpu_custom_call" | custom-call | flops 4000000000 | bytes 16000000 | tf_op jit(solution)/shard_map/filter/pallas_call | solution.py:525
  30.5 31.3 %reduce.1 = (f32[2,4,8,4224]{3,2,1,0:T(8,128)S(1)}, f32[32,2,4,128]{3,2,1,0:T(4,128)S(1)}) custom-call(f32[1024,256]{1,0:T(8,128)S(1)} %get-tuple-element.11.y0, f32[12,264,128]{2,1,0:T(8,128)S(1)} %get-tuple-element.12.sums_ref, bf16[256,256]{1,0:T(8,128)(2,1)S(1)} %get-tuple-element.13.wh, bf16[256,256]{1,0:T(8,128)(2,1)S(1)} %get-tuple-element.14.wl, ...), custom_call_target="tpu_custom_call" | custom-call | flops 400000000 | bytes 3000000 | tf_op jit(solution)/shard_map/reduce/pallas_call | solution.py:571
  61.8 0.0 copy-done
  61.9 4.0 %normalize.1 = (f32[4,4096]{1,0:T(4,128)}, f32[2,4,48,4096]{3,2,1,0:T(8,128)}) custom-call(s32[2,4]{1,0:T(2,128)S(1)} %bitcast.13, f32[256,128]{1,0:T(8,128)S(1)} %bitcast.12, f32[2,4,8,4224]{3,2,1,0:T(8,128)S(1)} %get-tuple-element.18.first_ref, f32[2,4,40,4224]{3,2,1,0:T(8,128)S(1)} %get-tuple-element.19.rest_ref), custom_call_target="tpu_custom_call" | custom-call | flops 2000000 | bytes 13000000 | tf_op jit(solution)/shard_map/normalize/pallas_call | solution.py:632
Async XLA Ops:
  0.6 1.0 %copy-start.1 = (f32[16,4096]{1,0:T(8,128)S(1)}, f32[16,4096]{1,0:T(8,128)}, u32[]{:S(2)}) copy-start(f32[16,4096]{1,0:T(8,128)} %param.4) | copy-start | bytes 786436
  1.6 60.3 %copy-start = (s32[4,2]{0,1:T(2,128)S(1)}, s32[4,2]{0,1:T(2,128)}, u32[]{:S(2)}) copy-start(s32[4,2]{0,1:T(2,128)} %param.5) | copy-start | bytes 100

commit v6 on v5

--- a/solution.py
+++ b/solution.py
@@ -136,26 +136,29 @@
     return lax.rem(i, 4) * 8 + i // 4
 
 
-def fir(refs, first, groups, tap0, tap1, extend=False):
-    (xf, tapb, y) = refs
+def fir(xf, tapb, first, parts, extend=False):
+    groups = len(parts)
+    lowest = min(p[0] for p in parts)
+    highest = max(p[1] for p in parts)
 
     def body(i, carry):
         base = i * PITCH + HALO + first * GROUP
         place = order_of(i)
         tap = {
-            t: tapb[pl.ds(pl.multiple_of((i * 16 + t) * 8, 8), 8), :] for t in range(tap0, tap1)
+            t: tapb[pl.ds(pl.multiple_of((i * 16 + t) * 8, 8), 8), :]
+            for t in range(lowest, highest)
         }
         for s in range(4):
             at = [
-                pl.ds(pl.multiple_of((g * 128 + s * 32 + place) * 8, 8), 8)
-                for g in range(groups)
+                pl.ds(pl.multiple_of((p[3] * 128 + s * 32 + place) * 8, 8), 8) for p in parts
             ]
             cols = [slice(c * LANES, (c + 1) * LANES) for c in range(2)]
             acc = [
-                [y[at[g], cols[c]] if extend else None for c in range(2)] for g in range(groups)
+                [p[2][at[g], cols[c]] if extend else None for c in range(2)]
+                for g, p in enumerate(parts)
             ]
-            for w in range(1 - tap1, 8 * (groups - 1) - tap0 + 1):
-                users = [g for g in range(groups) if tap0 <= 8 * g - w < tap1]
+            for w in range(1 - highest, 8 * (groups - 1) - lowest + 1):
+                users = [g for g, p in enumerate(parts) if p[0] <= 8 * g - w < p[1]]
                 if not users:
                     continue
                 x = [xf[2 * s + c, pl.ds(base + w, 8), :] for c in range(2)]
@@ -163,9 +166,9 @@
                     for c in range(2):
                         term = tap[8 * g - w] * x[c]
                         acc[g][c] = term if acc[g][c] is None else acc[g][c] + term
-            for g in range(groups):
+            for g, p in enumerate(parts):
                 for c in range(2):
-                    y[at[g], cols[c]] = acc[g][c]
+                    p[2][at[g], cols[c]] = acc[g][c]
         return carry
 
     lax.fori_loop(0, ROWS, body, 0)
@@ -209,7 +212,7 @@
 
     lax.fori_loop(0, 4 * groups, stage2a, 0)
 
-    def stage2b(n, carry):
+    def stage2b(n, carry, fresh=False):
         g = n // 8
         ka = lax.rem(n, 8)
         rows = tile(row_group + g)
@@ -241,7 +244,10 @@
                 pbuf[1, p, rows, cols] = im
         return carry
 
-    lax.fori_loop(0, 8 * groups, stage2b, 0)
+    if fresh:
+        lax.fori_loop(0, 8, functools.partial(stage2b, fresh=True), 0)
+    if groups > 1 or not fresh:
+        lax.fori_loop(8 if fresh else 0, 8 * groups, stage2b, 0)
 
 
 HALF = ROWS // 2
@@ -298,14 +304,14 @@
         ring, part, rows_in, _, _, _, sems = job
         d, e = ring.steps[n]
         return remote(
-            part.at[ring.member(d, e)], rows_in.at[n], sems.at[0, n], sems.at[1, n],
+            part.at[ring.member(d, e)], rows_in.at[n], sems.at[0], sems.at[1],
             ring.member_id(d, e),
         )
 
     def col_copy(job, n):
         ring, _, _, mine, cols_in, _, sems = job
         return remote(
-            mine, cols_in.at[n], sems.at[2, n], sems.at[3, n], ring.column_id(ring.shifts[n])
+            mine, cols_in.at[n], sems.at[2], sems.at[3], ring.column_id(ring.shifts[n])
         )
 
     def place(ring):
@@ -314,8 +320,18 @@
     def gather_copy(job, n):
         ring, _, _, _, _, stat, sems = job
         return remote(
-            stat, stats_ref.at[place(ring)], sems.at[4, n], sems.at[5, n],
+            stat, stats_ref.at[place(ring)], sems.at[4], sems.at[5],
             ring.member_id(*ring.steps[n]),
+        )
+
+    def whole(job, kind):
+        ring, _, rows_in, _, cols_in, _, sems = job
+        if kind == 2:
+            ref = stats_ref.at[pl.ds(0, (ring.members - 1) * ring.per)]
+        else:
+            ref = cols_in if kind else rows_in
+        return remote(
+            ref, ref, sems.at[2 * kind], sems.at[2 * kind + 1], ring.member_id(*ring.steps[0])
         )
 
     for job in work:
@@ -344,8 +360,8 @@
     for job in work:
         ring, part, rows_in, mine = job[:4]
         acc = part[ring.member()]
-        for n in reversed(range(len(ring.steps))):
-            row_copy(job, n).wait_recv()
+        whole(job, 0).wait_recv()
+        for n in range(len(ring.steps)):
             acc = acc + rows_in[n]
         mine[...] = acc
         for n in range(len(ring.shifts)):
@@ -354,8 +370,9 @@
 
     for job, acc in zip(work, totals):
         ring, _, _, _, cols_in, stat, _ = job
-        for n in reversed(range(len(ring.shifts))):
-            col_copy(job, n).wait_recv()
+        if ring.shifts:
+            whole(job, 1).wait_recv()
+        for n in range(len(ring.shifts)):
             acc = acc + cols_in[n]
         mean = acc * np.float32(1.0 / total)
         for r in range(ring.per):
@@ -372,16 +389,12 @@
         stats_ref[place(ring)] = stat[...]
 
     for job in work:
-        ring = job[0]
-        for n in reversed(range(len(ring.steps))):
-            gather_copy(job, n).wait_recv()
+        whole(job, 2).wait_recv()
     for job in work:
-        ring = job[0]
-        for n in range(len(ring.steps)):
-            row_copy(job, n).wait_send()
-            gather_copy(job, n).wait_send()
-        for n in range(len(ring.shifts)):
-            col_copy(job, n).wait_send()
+        whole(job, 0).wait_send()
+        if job[0].shifts:
+            whole(job, 1).wait_send()
+        whole(job, 2).wait_send()
 
 
 def filter_kernel(
@@ -445,9 +458,7 @@
         def _():
             halo_copy(b).wait_recv()
 
-    filters = (xf, tapb, y)
     refs = (y, wh, wl, twc, tws, v, u, prod_ref, sums)
-    sums[...] = jnp.zeros_like(sums)
     fill_tables(wh, wl, twc, tws)
     permute_taps(taps_ref, tapb)
 
@@ -458,23 +469,21 @@
 
     lax.fori_loop(0, 12, own_batch, 0)
 
-    fir(filters, 2, 4, 0, 16)
-    transform(refs, 1, 4)
+    fir(xf, tapb, 2, [(0, 16, y, g) for g in range(4)])
+    transform(refs, 1, 4, fresh=True)
 
     halo_wait(3)
     halo_wait(2)
     permute_batch(hraw, xf, 3, 0)
     permute_batch(hraw, xf, 2, 0)
-    fir(filters, 1, 1, 0, 16)
+    fir(xf, tapb, 0, [(0, 9, y0_ref, 0), (0, 16, y, 0)])
     transform(refs, 0, 1)
 
-    filters = (xf, tapb, y0_ref)
     halo_wait(1)
     permute_batch(hraw, xf, 1, 0)
-    fir(filters, 0, 1, 0, 13)
     halo_wait(0)
     permute_batch(hraw, xf, 0, 0)
-    fir(filters, 0, 1, 13, 16, extend=True)
+    fir(xf, tapb, 0, [(9, 16, y0_ref, 0)], extend=True)
 
     @pl.when(has_next)
     def _():
@@ -566,7 +575,7 @@
             pltpu.VMEM((ring.per, 3, 4, LANES), f32),
             pltpu.VMEM((max(ring.nb - 1, 1), ring.per, 3, 4, LANES), f32),
             pltpu.VMEM((ring.per, 2, 4, LANES), f32),
-            dma((6, max(ring.members, ring.nb) - 1)),
+            dma((6,)),
         ]
     return pl.pallas_call(
         functools.partial(reduce_kernel, total),

time: 66 us -> 64.3 us (0.974)
  Pallas kernels: 64.3 us -> 62.6 us
    pallas_call x1, Pallas kernels: 31.3 us -> 29.8 us  [reduce_call(): pl.pallas_call(functools.partial(reduce_kernel, total), out_shape=(jax.Sh...]
where the time goes in v6:
time: 64.3 us; the launch traced here: 64.2 us
  Pallas kernels  62.6 us (97%)
  local copies, waits for them, and re-layouts  0.95 us (1%)
  between operations  0.66 us (1%)
    pallas_call x1, Pallas kernels, reduce_call(): pl.pallas_call(functools.partial(reduce_kernel, total), out_shape=(jax.Sh...  29.8 us
    pallas_call x1, Pallas kernels, filter_call(): pl.pallas_call(filter_kernel, out_shape=(jax.ShapeDtypeStruct((2, 4, fram...  28.8 us
    pallas_call x1, Pallas kernels, normalize_call(): pl.pallas_call(normalize_kernel, in_specs=[pl.BlockSpec(memory_space=pltp...  4.01 us

profile of v6, /device:TPU:513, one launch (start us, length us, event | category | flops | bytes accessed | tf_op | source)
XLA Modules:
  0.0 64.2 jit_solution(13493690210857524408)
XLA Ops:
  0.6 0.0 copy-start.1
  0.6 0.9 %copy-done.1 = f32[16,4096]{1,0:T(8,128)S(1)} copy-done((f32[16,4096]{1,0:T(8,128)S(1)}, f32[16,4096]{1,0:T(8,128)}, u32[]{:S(2)}) %copy-start.1) | copy-done | bytes 262168
  1.6 0.0 copy-start
  1.6 28.8 %filter.1 = (f32[2,4,40,4224]{3,2,1,0:T(8,128)S(1)}, f32[1024,256]{1,0:T(8,128)S(1)}, f32[12,264,128]{2,1,0:T(8,128)S(1)}, bf16[256,256]{1,0:T(8,128)(2,1)S(1)},...) custom-call(s32[4,3072,128]{2,1,0:T(8,128)} %bitcast.15, f32[512,128]{1,0:T(8,128)S(1)} %bitcast.14), custom_call_target="tpu_custom_call" | custom-call | flops 4000000000 | bytes 16000000 | tf_op jit(solution)/shard_map/filter/pallas_call | solution.py:534
  30.3 29.8 %reduce.1 = (f32[2,4,8,4224]{3,2,1,0:T(8,128)S(1)}, f32[32,2,4,128]{3,2,1,0:T(4,128)S(1)}) custom-call(f32[1024,256]{1,0:T(8,128)S(1)} %get-tuple-element.11.y0, f32[12,264,128]{2,1,0:T(8,128)S(1)} %get-tuple-element.12.sums_ref, bf16[256,256]{1,0:T(8,128)(2,1)S(1)} %get-tuple-element.13.wh, bf16[256,256]{1,0:T(8,128)(2,1)S(1)} %get-tuple-element.14.wl, ...), custom_call_target="tpu_custom_call" | custom-call | flops 400000000 | bytes 3000000 | tf_op jit(solution)/shard_map/reduce/pallas_call | solution.py:580
  60.2 0.0 copy-done
  60.2 4.0 %normalize.1 = (f32[4,4096]{1,0:T(4,128)}, f32[2,4,48,4096]{3,2,1,0:T(8,128)}) custom-call(s32[2,4]{1,0:T(2,128)S(1)} %bitcast.13, f32[256,128]{1,0:T(8,128)S(1)} %bitcast.12, f32[2,4,8,4224]{3,2,1,0:T(8,128)S(1)} %get-tuple-element.18.first_ref, f32[2,4,40,4224]{3,2,1,0:T(8,128)S(1)} %get-tuple-element.19.rest_ref), custom_call_target="tpu_custom_call" | custom-call | flops 2000000 | bytes 13000000 | tf_op jit(solution)/shard_map/normalize/pallas_call | solution.py:641
Async XLA Ops:
  0.6 1.0 %copy-start.1 = (f32[16,4096]{1,0:T(8,128)S(1)}, f32[16,4096]{1,0:T(8,128)}, u32[]{:S(2)}) copy-start(f32[16,4096]{1,0:T(8,128)} %param.4) | copy-start | bytes 786436
  1.6 58.6 %copy-start = (s32[4,2]{0,1:T(2,128)S(1)}, s32[4,2]{0,1:T(2,128)}, u32[]{:S(2)}) copy-start(s32[4,2]{0,1:T(2,128)} %param.5) | copy-start | bytes 100

commit v7 on v6

--- a/solution.py
+++ b/solution.py
@@ -253,6 +253,10 @@
 HALF = ROWS // 2
 
 
+def turned(index, by, size):
+    return lax.rem(index + by, size) if by else index
+
+
 class Ring:
     def __init__(self, half, a, b):
         self.half, self.a, self.b, self.c = half, a, b, TM[2]
@@ -264,18 +268,17 @@
         self.shifts = sorted(range(1, self.nb), key=lambda d: -min(d, self.nb - d))
 
     def member(self, d=0, e=0):
-        at = lax.rem(lax.axis_index(self.a) + d, self.na)
-        core = lax.rem(lax.axis_index(self.c) + e, self.nc)
-        return at * self.nc + core
+        at = turned(lax.axis_index(self.a), d, self.na)
+        return at * self.nc + turned(lax.axis_index(self.c), e, self.nc)
 
     def member_id(self, d, e):
         return {
-            self.a: lax.rem(lax.axis_index(self.a) + d, self.na),
-            self.c: lax.rem(lax.axis_index(self.c) + e, self.nc),
+            self.a: turned(lax.axis_index(self.a), d, self.na),
+            self.c: turned(lax.axis_index(self.c), e, self.nc),
         }
 
     def column_id(self, d):
-        return {self.b: lax.rem(lax.axis_index(self.b) + d, self.nb)}
+        return {self.b: turned(lax.axis_index(self.b), d, self.nb)}
 
 
 def rings():
@@ -601,7 +604,9 @@
     )(y0, sums, *consts)
 
 
-def normalize_kernel(pairs_ref, stats_ref, first_ref, rest_ref, coh_ref, out_ref, buf, writes):
+def normalize_kernel(
+    pairs_ref, stats_ref, first_ref, rest_ref, coh_out, out_ref, buf, coh_ref, writes, coh_sem
+):
     frames = buf.shape[2]
 
     def write(p, part):
@@ -630,9 +635,12 @@
         value = stat(4 + pairs_ref[0, p] * 2 + pairs_ref[1, p] - 2)
         for k1 in range(ROWS):
             coh_ref[p : p + 1, k1 * LANES : (k1 + 1) * LANES] = value[k1 : k1 + 1]
+    coh_copy = pltpu.make_async_copy(coh_ref, coh_out, coh_sem)
+    coh_copy.start()
     for p in range(4):
         for part in range(2):
             write(p, part).wait()
+    coh_copy.wait()
 
 
 def normalize_call(pairs, stats, first, rest):
@@ -641,14 +649,16 @@
     return pl.pallas_call(
         normalize_kernel,
         in_specs=[pl.BlockSpec(memory_space=pltpu.SMEM)] + [VMEM_ALL] * 3,
-        out_specs=(VMEM_ALL, ANYWHERE),
+        out_specs=(ANYWHERE, ANYWHERE),
         out_shape=(
             jax.ShapeDtypeStruct((4, 4096), f32),
             jax.ShapeDtypeStruct((2, 4, frames, 4096), f32),
         ),
         scratch_shapes=[
             pltpu.VMEM((4, 2, frames, 4096), f32),
+            pltpu.VMEM((4, 4096), f32),
             pltpu.SemaphoreType.DMA((8,)),
+            pltpu.SemaphoreType.DMA,
         ],
         compiler_params=pltpu.CompilerParams(vmem_limit_bytes=20 * MIB),
         cost_estimate=pl.CostEstimate(flops=2_000_000, bytes_accessed=13_000_000, transcendentals=0),

time: 64.3 us -> 63.7 us (level)
  no operation moved by 1% of the time
where the time goes in v7:
time: 63.7 us; the launch traced here: 63.6 us
  Pallas kernels  62 us (97%)
  local copies, waits for them, and re-layouts  0.95 us (1%)
  between operations  0.66 us (1%)
    pallas_call x1, Pallas kernels, reduce_call(): pl.pallas_call(functools.partial(reduce_kernel, total), out_shape=(jax.Sh...  29.8 us
    pallas_call x1, Pallas kernels, filter_call(): pl.pallas_call(filter_kernel, out_shape=(jax.ShapeDtypeStruct((2, 4, fram...  28.8 us
    pallas_call x1, Pallas kernels, normalize_call(): pl.pallas_call(normalize_kernel, in_specs=[pl.BlockSpec(memory_space=pltp...  3.39 us

profile of v7, /device:TPU:513, one launch (start us, length us, event | category | flops | bytes accessed | tf_op | source)
XLA Modules:
  0.0 63.6 jit_solution(3546118760914300066)
XLA Ops:
  0.6 0.0 copy-start.1
  0.6 0.9 %copy-done.1 = f32[16,4096]{1,0:T(8,128)S(1)} copy-done((f32[16,4096]{1,0:T(8,128)S(1)}, f32[16,4096]{1,0:T(8,128)}, u32[]{:S(2)}) %copy-start.1) | copy-done | bytes 262168
  1.6 0.0 copy-start
  1.6 28.8 %filter.1 = (f32[2,4,40,4224]{3,2,1,0:T(8,128)S(1)}, f32[1024,256]{1,0:T(8,128)S(1)}, f32[12,264,128]{2,1,0:T(8,128)S(1)}, bf16[256,256]{1,0:T(8,128)(2,1)S(1)},...) custom-call(s32[4,3072,128]{2,1,0:T(8,128)} %bitcast.15, f32[512,128]{1,0:T(8,128)S(1)} %bitcast.14), custom_call_target="tpu_custom_call" | custom-call | flops 4000000000 | bytes 16000000 | tf_op jit(solution)/shard_map/filter/pallas_call | solution.py:537
  30.3 29.8 %reduce.1 = (f32[2,4,8,4224]{3,2,1,0:T(8,128)S(1)}, f32[32,2,4,128]{3,2,1,0:T(4,128)S(1)}) custom-call(f32[1024,256]{1,0:T(8,128)S(1)} %get-tuple-element.11.y0, f32[12,264,128]{2,1,0:T(8,128)S(1)} %get-tuple-element.12.sums_ref, bf16[256,256]{1,0:T(8,128)(2,1)S(1)} %get-tuple-element.13.wh, bf16[256,256]{1,0:T(8,128)(2,1)S(1)} %get-tuple-element.14.wl, ...), custom_call_target="tpu_custom_call" | custom-call | flops 400000000 | bytes 3000000 | tf_op jit(solution)/shard_map/reduce/pallas_call | solution.py:583
  60.2 0.0 copy-done
  60.2 3.4 %normalize.1 = (f32[4,4096]{1,0:T(4,128)}, f32[2,4,48,4096]{3,2,1,0:T(8,128)}) custom-call(s32[2,4]{1,0:T(2,128)S(1)} %bitcast.13, f32[256,128]{1,0:T(8,128)S(1)} %bitcast.12, f32[2,4,8,4224]{3,2,1,0:T(8,128)S(1)} %get-tuple-element.18.first_ref, f32[2,4,40,4224]{3,2,1,0:T(8,128)S(1)} %get-tuple-element.19.rest_ref), custom_call_target="tpu_custom_call" | custom-call | flops 2000000 | bytes 13000000 | tf_op jit(solution)/shard_map/normalize/pallas_call | solution.py:649
Async XLA Ops:
  0.6 1.0 %copy-start.1 = (f32[16,4096]{1,0:T(8,128)S(1)}, f32[16,4096]{1,0:T(8,128)}, u32[]{:S(2)}) copy-start(f32[16,4096]{1,0:T(8,128)} %param.4) | copy-start | bytes 786436
  1.6 58.6 %copy-start = (s32[4,2]{0,1:T(2,128)S(1)}, s32[4,2]{0,1:T(2,128)}, u32[]{:S(2)}) copy-start(s32[4,2]{0,1:T(2,128)} %param.5) | copy-start | bytes 100

commit v8 on v7

--- a/solution.py
+++ b/solution.py
@@ -354,10 +354,12 @@
                     ],
                     axis=0,
                 )
-        if ring.half == 0:
-            ready()
-        for n in range(len(ring.steps)):
-            row_copy(job, n).start()
+
+    ready()
+    for n in range(max(len(job[0].steps) for job in work)):
+        for job in work:
+            if n < len(job[0].steps):
+                row_copy(job, n).start()
 
     totals = []
     for job in work:

time: 63.7 us -> 63.5 us (level)
  no operation moved by 1% of the time
where the time goes in v8:
time: 63.5 us; the launch traced here: 63.4 us
  Pallas kernels  61.8 us (97%)
  local copies, waits for them, and re-layouts  0.95 us (1%)
  between operations  0.66 us (1%)
    pallas_call x1, Pallas kernels, reduce_call(): pl.pallas_call(functools.partial(reduce_kernel, total), out_shape=(jax.Sh...  29.6 us
    pallas_call x1, Pallas kernels, filter_call(): pl.pallas_call(filter_kernel, out_shape=(jax.ShapeDtypeStruct((2, 4, fram...  28.8 us
    pallas_call x1, Pallas kernels, normalize_call(): pl.pallas_call(normalize_kernel, in_specs=[pl.BlockSpec(memory_space=pltp...  3.39 us

profile of v8, /device:TPU:513, one launch (start us, length us, event | category | flops | bytes accessed | tf_op | source)
XLA Modules:
  0.0 63.4 jit_solution(11190435912715200701)
XLA Ops:
  0.6 0.0 copy-start.1
  0.6 0.9 %copy-done.1 = f32[16,4096]{1,0:T(8,128)S(1)} copy-done((f32[16,4096]{1,0:T(8,128)S(1)}, f32[16,4096]{1,0:T(8,128)}, u32[]{:S(2)}) %copy-start.1) | copy-done | bytes 262168
  1.6 0.0 copy-start
  1.6 28.8 %filter.1 = (f32[2,4,40,4224]{3,2,1,0:T(8,128)S(1)}, f32[1024,256]{1,0:T(8,128)S(1)}, f32[12,264,128]{2,1,0:T(8,128)S(1)}, bf16[256,256]{1,0:T(8,128)(2,1)S(1)},...) custom-call(s32[4,3072,128]{2,1,0:T(8,128)} %bitcast.15, f32[512,128]{1,0:T(8,128)S(1)} %bitcast.14), custom_call_target="tpu_custom_call" | custom-call | flops 4000000000 | bytes 16000000 | tf_op jit(solution)/shard_map/filter/pallas_call | solution.py:539
  30.3 29.6 %reduce.1 = (f32[2,4,8,4224]{3,2,1,0:T(8,128)S(1)}, f32[32,2,4,128]{3,2,1,0:T(4,128)S(1)}) custom-call(f32[1024,256]{1,0:T(8,128)S(1)} %get-tuple-element.11.y0, f32[12,264,128]{2,1,0:T(8,128)S(1)} %get-tuple-element.12.sums_ref, bf16[256,256]{1,0:T(8,128)(2,1)S(1)} %get-tuple-element.13.wh, bf16[256,256]{1,0:T(8,128)(2,1)S(1)} %get-tuple-element.14.wl, ...), custom_call_target="tpu_custom_call" | custom-call | flops 400000000 | bytes 3000000 | tf_op jit(solution)/shard_map/reduce/pallas_call | solution.py:585
  60.0 0.0 copy-done
  60.0 3.4 %normalize.1 = (f32[4,4096]{1,0:T(4,128)}, f32[2,4,48,4096]{3,2,1,0:T(8,128)}) custom-call(s32[2,4]{1,0:T(2,128)S(1)} %bitcast.13, f32[256,128]{1,0:T(8,128)S(1)} %bitcast.12, f32[2,4,8,4224]{3,2,1,0:T(8,128)S(1)} %get-tuple-element.18.first_ref, f32[2,4,40,4224]{3,2,1,0:T(8,128)S(1)} %get-tuple-element.19.rest_ref), custom_call_target="tpu_custom_call" | custom-call | flops 2000000 | bytes 13000000 | tf_op jit(solution)/shard_map/normalize/pallas_call | solution.py:651
Async XLA Ops:
  0.6 1.0 %copy-start.1 = (f32[16,4096]{1,0:T(8,128)S(1)}, f32[16,4096]{1,0:T(8,128)}, u32[]{:S(2)}) copy-start(f32[16,4096]{1,0:T(8,128)} %param.4) | copy-start | bytes 786436
  1.6 58.4 %copy-start = (s32[4,2]{0,1:T(2,128)S(1)}, s32[4,2]{0,1:T(2,128)}, u32[]{:S(2)}) copy-start(s32[4,2]{0,1:T(2,128)} %param.5) | copy-start | bytes 100
